TPU v7x, 512 devices: a whole 4x8x8 slice. The times are simulated.
512 devices in a mesh: cls: 8 (over y_hi, core), img: 64 (over y_lo, z, x).
Axes of the slice: x: 4, y: 8 (y_hi: 4, y_lo: 2; y = y_hi * 2 + y_lo), z: 8, core: 2. Of those that a mesh axis runs over, the one named last changes fastest.
Arguments:
- images: bfloat16 [28672, 7200], P(('cls', 'img')), may hold values from -8 to 8
- projections: bfloat16 [1024, 7200], P('cls'), may hold values from -0.42426407 to 0.42426407
- noise_power: float32 [32, 7200], replicated, may hold values from 0.5 to 4
- class_logprior: float32 [4], replicated, may hold values from -1.5 to 1.5
- groups: int32 [28672], P(('cls', 'img')), may hold values from 0 to 31
- offsets: int32 [28672], P(('cls', 'img')), may hold values from 0 to 3
Outputs:
- weighted_sums: float32 [1024, 7200], P(('cls', 'img'))
- log_evidence: float32 [28672], P(('cls', 'img'))
All inputs are finite; a program needn't handle non-finite values.
Results may differ from a plain program's by a relative error of at most 0.0064.
Values may be sent and summed in bfloat16 or wider, within the bound.
A program may use at most 64 MiB of HBM per device.

v0:
```python
import jax
import jax.numpy as jnp
from jax import lax
from jax.sharding import PartitionSpec as P


def side_by_side(arrays, axis, dim, along):
    ends, at = ([], 0)
    for a in arrays[:-1]:
        at += a.shape[along]
        ends.append(at)
    both = jnp.concatenate(arrays, axis=along)
    return tuple(jnp.split(lax.all_gather(both, axis, axis=dim, tiled=True), ends, axis=along))


def copy_for_each(array, axis):
    copies = jnp.broadcast_to(array, (lax.axis_size(axis), *array.shape))
    return lax.all_to_all(copies, axis, split_axis=0, concat_axis=0, tiled=True)


def all_in_one(array, axis):
    leaves = jax.tree.leaves(array)
    sequence = sorted(range(len(leaves)), key=lambda k: -leaves[k].size)
    width = (1, *leaves[sequence[0]].shape)[-1]
    lines = [
        jnp.pad(leaves[k].reshape(-1), (0, -leaves[k].size % width)).reshape(-1, width)
        for k in sequence
    ]
    both, at, found = (copy_for_each(jnp.concatenate(lines), axis), 0, {})
    for k, line in zip(sequence, lines):
        section = both[:, at : at + len(line)].reshape(len(both), -1)
        found[k] = section[:, : leaves[k].size].reshape(-1, *leaves[k].shape)
        at += len(line)
    numbers = iter(range(len(leaves)))
    return jax.tree.map(lambda _: found[next(numbers)], array)


def joined_by_halves(pieces, combine):
    while len(jax.tree.leaves(pieces)[0]) > 1:
        pieces = jax.vmap(combine)(
            *(jax.tree.map(lambda part: part[side::2], pieces) for side in (0, 1))
        )
    return jax.tree.map(lambda part: part[0], pieces)


def joined_all(array, axis, combine):
    pieces = all_in_one(array, axis)
    return joined_by_halves(pieces, combine)


def in_blocks(array, dim, devices):
    shape = array.shape
    parts = array.reshape(*shape[:dim], devices, shape[dim] // devices, *shape[dim + 1 :])
    return jnp.moveaxis(parts, dim, 0)


def summed_on_arrival(array, axis, dim):
    parts = in_blocks(array, dim, lax.axis_size(axis))
    arrived = lax.all_to_all(parts, axis, split_axis=0, concat_axis=0, tiled=True)
    return arrived.astype(jnp.float32).sum(axis=0)


def merge_parts(first, second):
    peak = jnp.maximum(first[0], second[0])
    return (peak, first[1] * jnp.exp(first[0] - peak) + second[1] * jnp.exp(second[0] - peak))


def body(images, projections, noise_power, class_logprior, groups, offsets):
    rows_here = images.shape[0]
    proj_here = projections.shape[0]
    cycle_size = lax.axis_size("cls")
    cycle_place = lax.axis_index("cls")
    group_count = noise_power.shape[0]
    class_count = class_logprior.shape[0]
    inverse = 1.0 / noise_power
    group_hot = (groups[:, None] == jnp.arange(group_count, dtype=jnp.int32)[None, :]).astype(
        jnp.float32
    )
    offset_hot = (offsets[:, None] == jnp.arange(class_count, dtype=jnp.int32)[None, :]).astype(
        jnp.float32
    )
    row_inverse = jnp.dot(group_hot, inverse, precision=lax.Precision.HIGHEST)
    whitened = (images.astype(jnp.float32) * row_inverse).astype(jnp.bfloat16)
    tag_rows = jnp.concatenate([group_hot, offset_hot], axis=1).astype(jnp.bfloat16)
    proj_float = projections.astype(jnp.float32)
    quadratic = jnp.dot(inverse, (proj_float * proj_float).T, precision=lax.Precision.HIGHEST)
    global_index = cycle_place * proj_here + jnp.arange(proj_here, dtype=jnp.int32)
    per_class = proj_here * cycle_size // class_count
    class_of = global_index // per_class
    class_shift = (
        class_of[None, :] - jnp.arange(class_count, dtype=jnp.int32)[:, None]
    ) % class_count
    matches = class_shift[:, :, None] == jnp.arange(class_count, dtype=jnp.int32)[None, None, :]
    prior_table = jnp.sum(jnp.where(matches, class_logprior[None, None, :], 0.0), axis=2)
    bias_table = jnp.concatenate([-0.5 * quadratic, prior_table], axis=0)
    gathered, labels = side_by_side((whitened, tag_rows), "cls", 0, 1)
    products = jnp.einsum("bf,pf->bp", gathered, projections, preferred_element_type=jnp.float32)
    scores = products + jnp.dot(
        labels.astype(jnp.float32), bias_table, precision=lax.Precision.HIGHEST
    )
    local_peak = jnp.max(scores, axis=1)
    local_sum = jnp.sum(jnp.exp(scores - local_peak[:, None]), axis=1)
    peak, exp_sum = joined_all((local_peak, local_sum), "cls", merge_parts)
    evidence = peak + jnp.log(exp_sum)
    posterior = jnp.exp(scores - evidence[:, None]).astype(jnp.bfloat16)
    sum_rows = summed_on_arrival(
        jnp.einsum("bp,bf->pf", posterior, gathered, preferred_element_type=jnp.float32).astype(
            jnp.bfloat16
        ),
        "img",
        0,
    )
    own_evidence = lax.dynamic_slice_in_dim(evidence, cycle_place * rows_here, rows_here)
    return (sum_rows, own_evidence)


def solution(mesh):
    in_specs = (
        P(("cls", "img"), None),
        P("cls", None),
        P(),
        P(),
        P(("cls", "img")),
        P(("cls", "img")),
    )
    out_specs = (P(("cls", "img"), None), P(("cls", "img")))
    return jax.shard_map(body, mesh=mesh, in_specs=in_specs, out_specs=out_specs, check_vma=False)
```

profile of v0, /device:TPU:64, one launch (start us, length us, event | category | flops | bytes accessed | tf_op | source)
XLA Modules:
  0.0 186.2 jit_solution(8766484227556606067)
XLA Ops:
  7.2 0.0 all-gather.2.cloned.1.call-start
  7.2 0.7 iota_compare_fusion
  7.9 0.7 iota_compare_fusion.1
  8.7 0.1 convert_convert_fusion
  8.8 0.0 copy-start.2
  8.8 2.4 %fusion = bf16[56,7200]{1,0:T(8,128)(2,1)S(1)} fusion(bf16[56,7200]{1,0:T(8,128)(2,1)} %param.6, f32[32,7200]{1,0:T(8,128)} %param.8, s32[56]{0:T(128)} %param.10), kind=kOutput, calls=%fused_computation.2 | convolution fusion | flops 156270592 | bytes 2534624 | tf_op jit(solution)/shard_map/dot_general | solution.py:82
  11.2 0.0 copy-start
  11.2 0.0 copy-start.1
  11.2 1.0 pad_maximum_fusion
  12.2 0.0 all-gather.2.cloned.1.call-update
  12.3 0.0 copy-done
  12.3 0.1 select_reduce_fusion
  12.4 0.0 copy-done.2
  12.4 0.6 copy-done.1
  13.0 2.3 %fusion.7 = f32[32,128]{1,0:T(8,128)S(1)} fusion(bf16[128,7200]{0,1:T(8,128)(2,1)S(1)} %copy-done.1, f32[32,7200]{1,0:T(8,128)S(1)} %copy-done.2), kind=kOutput, calls=%fused_computation.11 | convolution fusion | flops 355972096 | bytes 2781184 | tf_op jit(solution)/shard_map/dot_general | solution.py:86
  15.3 73.3 %all-gather.2.cloned.1.call-done = bf16[448,7236]{1,0:T(8,128)(2,1)} async-done(((bf16[56,7236]{1,0:T(8,128)(2,1)}), bf16[448,7236]{1,0:T(8,128)(2,1)}) %all-gather.2.cloned.1.call-update) | async-done | bytes 6483472 | tf_op jit(solution)/shard_map/all_gather | solution.py:13
  88.6 4.7 %fusion.2 = f32[448,128]{1,0:T(8,128)S(1)} fusion(bf16[128,7200]{0,1:T(8,128)(2,1)S(1)} %copy-done.1, bf16[448,7236]{1,0:T(8,128)(2,1)} %all-gather.2.cloned.1.call-done), kind=kOutput, calls=%fused_computation.4 | convolution fusion | flops 825753600 | bytes 8556032 | tf_op jit(solution)/shard_map/bf,pf->bp/dot_general | solution.py:97
  93.4 1.3 fusion.22
  94.7 0.3 exponential_reduce_fusion
  94.9 13.9 %all_to_all.10 = f32[8,2,448]{2,1,0:T(2,128)S(1)} all-to-all(f32[8,2,448]{2,1,0:T(2,128)S(1)} %broadcast_in_dim.12), channel_id=1, replica_groups=mesh['cls'=8,'img'=64] {'cls'}, dimensions={0} | all-to-all | bytes 57344 | tf_op jit(solution)/shard_map/all_to_all | solution.py:18
  109.1 7.2 %convolution_convert_fusion = bf16[128,7200]{0,1:T(8,128)(2,1)} fusion(bf16[448,7236]{1,0:T(8,128)(2,1)} %all-gather.2.cloned.1.call-done, f32[448,128]{1,0:T(8,128)S(1)} %get-tuple-element.9, f32[448]{0:T(512)S(1)} %bitcast.12), kind=kOutput, calls=%fused_computation | convolution fusion | flops 826789888 | bytes 8557824 | tf_op jit(solution)/shard_map/bp,bf->pf/dot_general | solution.py:107
  116.3 2.8 %copy.12 = bf16[128,7200]{1,0:T(8,128)(2,1)S(1)} copy(bf16[128,7200]{0,1:T(8,128)(2,1)} %convolution_convert_fusion) | data formatting | bytes 3686400 | tf_op jit(solution)/shard_map/convert_element_type | solution.py:107
  119.1 1.7 reshape.89
  120.8 11.3 %all-to-all-start.1 = ((bf16[64,2,7200]{2,1,0:T(2,128)(2,1)}), bf16[64,2,7200]{2,1,0:T(2,128)(2,1)S(1)}, u32[]{:S(2)}, u32[]{:S(2)}) async-start(bf16[64,2,7200]{2,1,0:T(2,128)(2,1)} %reshape.89), calls=%async_computation.1 | async-start | bytes 3735552 | tf_op jit(solution)/shard_map/all_to_all | solution.py:59
  132.1 0.6 dynamic-slice_bitcast_fusion
  132.7 44.5 %all-to-all-done.1 = bf16[64,2,7200]{2,1,0:T(2,128)(2,1)S(1)} async-done(((bf16[64,2,7200]{2,1,0:T(2,128)(2,1)}), bf16[64,2,7200]{2,1,0:T(2,128)(2,1)S(1)}, u32[]{:S(2)}, u32[]{:S(2)}) %all-to-all-start.1) | async-done | bytes 1843232 | tf_op jit(solution)/shard_map/all_to_all | solution.py:59
  177.2 2.1 %convert_reduce_fusion = f32[2,7200]{1,0:T(2,128)} fusion(bf16[64,2,7200]{2,1,0:T(2,128)(2,1)S(1)} %all-to-all-done.1), kind=kLoop, calls=%fused_computation.6 | loop fusion | flops 1828800 | bytes 1900800 | tf_op jit(solution)/shard_map/reduce_sum | solution.py:60
  (17 shorter events, 0.3 us)
Async XLA Ops:
  7.2 81.5 %all-gather.2.cloned.1.call-start = ((), (), s32[]{:S(2)}) async-start(), calls=%async_computation.2 | async-start | bytes 7354368 | tf_op jit(solution)/shard_map/all_gather | solution.py:13
  8.8 3.6 %copy-start.2 = (f32[32,7200]{1,0:T(8,128)S(1)}, f32[32,7200]{1,0:T(8,128)}, u32[]{:S(2)}) copy-start(f32[32,7200]{1,0:T(8,128)} %param.8) | copy-start | bytes 2764804
  11.2 1.1 copy-start
  11.2 1.8 copy-start.1
  120.8 56.4 %all-to-all-start.1 = ((bf16[64,2,7200]{2,1,0:T(2,128)(2,1)}), bf16[64,2,7200]{2,1,0:T(2,128)(2,1)S(1)}, u32[]{:S(2)}, u32[]{:S(2)}) async-start(bf16[64,2,7200]{2,1,0:T(2,128)(2,1)} %reshape.89), calls=%async_computation.1 | async-start | bytes 3735552 | tf_op jit(solution)/shard_map/all_to_all | solution.py:59
Sparse Core Ops, SparseCore 0:
  12.4 76.2 all-gather.1
where the time goes:
time: 187 us; the launch traced here: 186 us
  waiting for transfers between devices  118 us (63%)
  matrix products  17.9 us (10%)
  between operations  14.2 us (8%)
  blocking collectives  13.9 us (7%)
  starting transfers between devices  11.4 us (6%)
  local copies, waits for them, and re-layouts  5.91 us (3%)
  other arithmetic  5.1 us (3%)
    all_gather x1, waiting for transfers between devices, side_by_side(): lax.all_gather(both, axis, axis=dim, tiled=True)  73.3 us
    all_to_all x1, waiting for transfers between devices, summed_on_arrival(): lax.all_to_all(parts, axis, split_axis=0, concat_axis=0, tiled=True)  44.5 us
    all_to_all x1, blocking collectives, copy_for_each(): return lax.all_to_all(copies, axis, split_axis=0, concat_axis=0, tiled=True)  13.9 us
    all_to_all x1, starting transfers between devices, summed_on_arrival(): lax.all_to_all(parts, axis, split_axis=0, concat_axis=0, tiled=True)  11.3 us
    dot_general x1, matrix products, body(): jnp.einsum('bp,bf->pf', posterior, gathered, preferred_element_type=jnp.f...  7.22 us
    dot_general x1, matrix products, body(): jnp.einsum('bf,pf->bp', gathered, projections, preferred_element_type=jnp...  4.71 us
  transfers between devices with their start and end apart: 2, of which 2 were waited for; matrix products, arithmetic and copies ran while one was open for 2% of the time, Pallas kernels for 0%

commit v1 on v0

v1 whole, which is shorter than its diff:
```python
import jax
import jax.numpy as jnp
from jax import lax
from jax.experimental import pallas as pl
from jax.experimental.pallas import tpu as pltpu
from jax.sharding import PartitionSpec as P

NX, NY, NZ = 4, 8, 8
F = 7200
W = 1920
TAG = 128
ROWS = 56
BLOCK = 128
CHUNKS = 4
CHUNK = BLOCK // CHUNKS
WA = 1024
WB = W - WA
GROUPS = 32
CLASSES = 4
OWN = 8
R_ORDER = (0, 1, 2, 3)
L_ORDER = (2, 3, 0, 1)
NT = (((1,), (1,)), ((), ()))
TN = (((0,), (0,)), ((), ()))
f32 = jnp.float32
bf16 = jnp.bfloat16


def kernel(
    img_ref, proj_ref, inv_ref, prior_ref, out_ref, ev_ref,
    xin, white, inv3, pbuf, qbuf, sc_send, sc_recv, post_send, post_recv,
    sum_a, sum_b, r1a, r1b, mid_a, mid_b, r2a, r2b, fin_send, fin_recv,
    img_s, img_r, ring_s, ring_r, sc_s, sc_r, post_s, post_r, rs_s, rs_r, fin_s, fin_r,
):
    cls = lax.axis_index("cls")
    img = lax.axis_index("img")
    h, c = cls // 2, cls % 2
    lo, z, x = img // (NZ * NX), (img // NX) % NZ, img % NX
    y = 2 * h + lo

    def device(y_, z_, x_, c_):
        return {"cls": (y_ // 2) * 2 + c_, "img": ((y_ % 2) * NZ + z_) * NX + x_}

    def group(dx, dc):
        return device(y, z, (x + dx) % NX, (c + dc) % 2)

    def along_y(d):
        return device((y + d) % NY, z, x, c)

    def along_z(d):
        return device(y, (z + d) % NZ, x, c)

    def copy(src, dst, send, recv, to):
        return pltpu.make_async_remote_copy(
            src_ref=src, dst_ref=dst, send_sem=send, recv_sem=recv,
            device_id=to, device_id_type=pl.DeviceIdType.MESH,
        )

    barrier = pltpu.get_barrier_semaphore()
    partners = [group(s // 2, s % 2) for s in range(1, 2 * NX)]
    partners += [along_y(d) for d in range(1, NY)] + [along_z(d) for d in range(1, NZ)]
    for to in partners:
        pl.semaphore_signal(barrier, inc=1, device_id=to, device_id_type=pl.DeviceIdType.MESH)
    pl.semaphore_wait(barrier, len(partners))

    def ring(way, m, src, rel, chunk):
        return copy(
            src, pbuf.at[rel, chunk], ring_s.at[way, m], ring_r.at[way, m],
            along_y(1 if way == 0 else NY - 1),
        )

    def ring_slot(way, m):
        order = R_ORDER if way == 0 else L_ORDER
        if m < CHUNKS:
            return (3 if way == 0 else 1), order[m]
        return 2, order[m - CHUNKS]

    for way in (0, 1):
        @pl.when(lo == 1 - way)
        def _(way=way):
            for m in range(CHUNKS):
                rel, chunk = ring_slot(way, m)
                ring(way, m, proj_ref.at[chunk], rel, chunk).start()

    def image(dx):
        return copy(
            img_ref.at[(x + dx) % NX], xin.at[2 * dx], img_s.at[2 * dx], img_r.at[2 * dx],
            group(dx, 0),
        )

    def to_sibling(dx):
        src = img_ref.at[x] if dx == 0 else xin.at[2 * dx]
        s = 2 * dx + 1
        return copy(src, xin.at[s], img_s.at[s], img_r.at[s], group(0, 1))

    for dx in (2, 1, 3):
        image(dx).start()
    to_sibling(0).start()
    xin[0] = img_ref[x]

    inv = inv_ref[...]
    hi = inv.astype(bf16)
    rest = inv - hi.astype(f32)
    mid = rest.astype(bf16)
    low = (rest - mid.astype(f32)).astype(bf16)
    inv3[0:GROUPS] = hi
    inv3[GROUPS : 2 * GROUPS] = mid
    inv3[2 * GROUPS : 3 * GROUPS] = low
    inv3[3 * GROUPS :] = jnp.zeros((TAG - 3 * GROUPS, W), bf16)

    lane = lax.broadcasted_iota(jnp.int32, (BLOCK, TAG), 1)
    piece = jnp.where(lane < 96, lane // 32, jnp.minimum((lane - 96) // 4, 3))

    def block_of(rel):
        return (proj_ref if rel == 0 else pbuf.at[rel])[...].reshape(BLOCK, W)

    def columns(rel):
        p = block_of(rel).astype(f32)
        square = p * p
        s_hi = square.astype(bf16)
        s_lo = (square - s_hi.astype(f32)).astype(bf16)
        q = lax.dot_general(s_hi, inv3[...], NT, preferred_element_type=f32)
        q += lax.dot_general(s_lo, inv3[...], NT, preferred_element_type=f32)
        q = q + pltpu.roll(q, 32, 1) + pltpu.roll(q, 64, 1) + pltpu.roll(q, 96, 1)
        value = jnp.where(lane < 96, -0.5 * q, prior_ref[rel : rel + 1, :])
        v_hi = value.astype(bf16).astype(f32)
        v_mid = (value - v_hi).astype(bf16).astype(f32)
        v_lo = value - v_hi - v_mid
        both = jnp.where(piece == 0, v_hi, jnp.where(piece == 1, v_mid, jnp.where(piece == 2, v_lo, 0.0)))
        qbuf[rel] = both.astype(bf16)

    def arrived(way, m):
        rel, chunk = ring_slot(way, m)
        ring(way, m, pbuf.at[rel, chunk], rel, chunk).wait_recv()

        @pl.when(lo == way)
        def _():
            ring(way, m, pbuf.at[rel, chunk], rel, chunk).start()

        if m < 2:
            @pl.when(lo == 1 - way)
            def _():
                ring(way, CHUNKS + m, pbuf.at[rel, chunk], 2, chunk).start()

    def image_arrived(dx):
        image(dx).wait_recv()
        to_sibling(dx).start()

    def score_copy(rel, s):
        return copy(
            sc_send.at[rel, s], sc_recv.at[rel, s], sc_s.at[rel, s], sc_r.at[rel, s],
            group((NX - s // 2) % NX, s % 2),
        )

    def scores(rel):
        columns(rel)
        tags = xin[:, :, W:].reshape(2 * NX * ROWS, TAG)
        part = lax.dot_general(
            white[...].reshape(2 * NX * ROWS, W), block_of(rel), NT, preferred_element_type=f32
        )
        part += lax.dot_general(tags, qbuf[rel], NT, preferred_element_type=f32)
        sc_send[rel] = part.reshape(2 * NX, ROWS, BLOCK)
        for s in (4, 5, 2, 3, 6, 7, 1):
            score_copy(rel, s).start()

    def whiten(s):
        inverse = jnp.dot(xin[s, :, W:], inv3[...], preferred_element_type=f32)
        white[s] = (xin[s, :, :W].astype(f32) * inverse).astype(bf16)

    whiten(0)
    arrived(0, 0)
    arrived(1, 0)
    image_arrived(1)
    image_arrived(3)
    arrived(0, 1)
    arrived(1, 1)
    image_arrived(2)
    for s in (2, 6, 4):
        whiten(s)
    arrived(0, 2)
    arrived(1, 2)
    for s in (1, 3, 7, 5):
        to_sibling(s // 2).wait_recv()
        whiten(s)
    scores(0)
    arrived(0, 3)
    arrived(1, 3)
    scores(3)
    arrived(0, 4)
    arrived(1, 4)
    scores(1)
    arrived(0, 5)
    arrived(1, 5)
    scores(2)

    total = {}
    for rel in (0, 3, 1, 2):
        for s in range(1, 2 * NX):
            score_copy(rel, s).wait_recv()
        for dc in (0, 1):
            parts = [sc_send[rel, 0]] if dc == 0 else [sc_recv[rel, 1]]
            parts += [sc_recv[rel, 2 * dx + dc] for dx in range(1, NX)]
            total[rel, dc] = (parts[0] + parts[1]) + (parts[2] + parts[3])
    peak = None
    for value in total.values():
        peak = value if peak is None else jnp.maximum(peak, value)
    peak = jnp.max(peak, axis=1, keepdims=True)
    mass = None
    for value in total.values():
        term = jnp.exp(value - peak)
        mass = term if mass is None else mass + term
    evidence = peak + jnp.log(jnp.sum(mass, axis=1, keepdims=True))
    ev_ref[...] = evidence
    for (rel, dc), value in total.items():
        post_send[dc, rel] = jnp.exp(value - evidence).astype(bf16)

    def post_copy(s):
        return copy(
            post_send.at[s % 2], post_recv.at[s], post_s.at[s], post_r.at[s], group(s // 2, s % 2)
        )

    for s in (4, 5, 2, 3, 6, 7, 1):
        post_copy(s).start()
    post_recv[0] = post_send[0]
    for s in (1, 2, 3, 6, 7, 4, 5):
        post_copy(s).wait_recv()

    def weights(rel):
        return post_recv[:, rel].reshape(2 * NX * ROWS, BLOCK)

    def rs(which, d, src, dst, to):
        return copy(src, dst, rs_s.at[which, d], rs_r.at[which, d], to)

    def first_b(d):
        return rs(0, d, sum_b.at[(lo + d) % NY], r1b.at[d], along_y(d))

    def first_a(d):
        return rs(1, d, sum_a.at[(z + d) % NZ], r1a.at[d], along_z(d))

    def second_b(d):
        return rs(2, d, mid_b.at[(z + d) % NZ], r2b.at[d], along_z(d))

    def second_a(d):
        return rs(3, d, mid_a.at[(lo + d) % NY], r2a.at[d], along_y(d))

    far_first = (4, 3, 5, 2, 6, 1, 7)
    near_first = (1, 7, 2, 6, 3, 5, 4)
    for rel in range(4):
        part = lax.dot_general(
            weights(rel), white[:, :, WA:].reshape(2 * NX * ROWS, WB), TN, preferred_element_type=f32
        ).astype(bf16)
        for r in range(2 * NZ):
            sum_b[2 * rel + r // NZ, r % NZ] = part[OWN * r : OWN * (r + 1)]
    for d in far_first:
        first_b(d).start()
    for rel in range(4):
        part = lax.dot_general(
            weights(rel), white[:, :, :WA].reshape(2 * NX * ROWS, WA), TN, preferred_element_type=f32
        ).astype(bf16)
        for r in range(2 * NZ):
            sum_a[r % NZ, 2 * rel + r // NZ] = part[OWN * r : OWN * (r + 1)]
    for d in far_first:
        first_a(d).start()

    for d in near_first:
        first_b(d).wait_recv()
    for q in range(NZ):
        acc = sum_b[lo, q].astype(f32)
        for d in range(1, NY):
            acc += r1b[d, q].astype(f32)
        mid_b[q] = acc.astype(bf16)
    for d in far_first:
        second_b(d).start()
    for d in near_first:
        first_a(d).wait_recv()
    for q in range(NY):
        acc = sum_a[z, q].astype(f32)
        for d in range(1, NZ):
            acc += r1a[d, q].astype(f32)
        mid_a[q] = acc.astype(bf16)
    for d in far_first:
        second_a(d).start()

    for d in near_first:
        second_b(d).wait_recv()
    acc_b = mid_b[z].astype(f32)
    for d in range(1, NZ):
        acc_b += r2b[d].astype(f32)
    for d in near_first:
        second_a(d).wait_recv()
    acc_a = mid_a[lo].astype(f32)
    for d in range(1, NY):
        acc_a += r2a[d].astype(f32)

    def fin(d):
        return copy(
            fin_send.at[(x + d) % NX], fin_recv.at[x], fin_s.at[d], fin_r.at[d], group(d, 0)
        )

    def fin_in(d):
        return copy(
            fin_send.at[x], fin_recv.at[(x + NX - d) % NX], fin_s.at[d], fin_r.at[d], group(d, 0)
        )

    for k in range(NX):
        fin_send[k, :, :WA] = acc_a[2 * k : 2 * k + 2]
        fin_send[k, :, WA:] = acc_b[2 * k : 2 * k + 2]
    for d in (2, 1, 3):
        fin(d).start()
    fin_recv[x] = fin_send[x]
    for d in (1, 3, 2):
        fin_in(d).wait_recv()
    for k in range(NX):
        end = min(F, W * (k + 1))
        out_ref[:, W * k : end] = fin_recv[k, :, : end - W * k]

    for way in (0, 1):
        for m in range(6):
            rel, chunk = ring_slot(way, m)
            ring(way, m, pbuf.at[rel, chunk], rel, chunk).wait_send()
    for dx in range(NX):
        if dx:
            image(dx).wait_send()
        to_sibling(dx).wait_send()
    for s in range(1, 2 * NX):
        for rel in range(4):
            score_copy(rel, s).wait_send()
        post_copy(s).wait_send()
    for d in range(1, NY):
        first_a(d).wait_send()
        first_b(d).wait_send()
        second_a(d).wait_send()
        second_b(d).wait_send()
    for d in range(1, NX):
        fin(d).wait_send()


def body(images, projections, noise_power, class_logprior, groups, offsets):
    h = lax.axis_index("cls") // 2
    x = lax.axis_index("img") % NX
    lane = jnp.arange(TAG, dtype=jnp.int32)[None, :]
    is_group = (lane < 96) & (lane % 32 == groups[:, None])
    is_offset = (lane >= 96) & (lane < 108) & (lane % 4 == offsets[:, None])
    tags = (is_group | is_offset).astype(bf16)
    cut = jnp.pad(images, ((0, 0), (0, NX * W - F))).reshape(ROWS, NX, W)
    cut = jnp.concatenate([cut, jnp.broadcast_to(tags[:, None, :], (ROWS, NX, TAG))], axis=2)
    cut = jnp.transpose(cut, (1, 0, 2))
    mine = lax.dynamic_slice_in_dim(
        jnp.pad(projections, ((0, 0), (0, NX * W - F))), x * W, W, axis=1
    ).reshape(CHUNKS, CHUNK, W)
    noise = lax.dynamic_slice_in_dim(
        jnp.pad(noise_power, ((0, 0), (0, NX * W - F)), constant_values=1.0), x * W, W, axis=1
    )
    rel = jnp.arange(4, dtype=jnp.int32)[:, None]
    place = (h + rel + 128 - lane) % CLASSES
    prior = sum(jnp.where(place == n, class_logprior[n], 0.0) for n in range(CLASSES)) * (1.0 / NX)
    dma = pltpu.SemaphoreType.DMA
    out, evidence = pl.pallas_call(
        kernel,
        out_shape=(
            jax.ShapeDtypeStruct((2, F), f32),
            jax.ShapeDtypeStruct((ROWS, 1), f32),
        ),
        in_specs=[pl.BlockSpec(memory_space=pltpu.VMEM)] * 4,
        out_specs=(pl.BlockSpec(memory_space=pltpu.VMEM),) * 2,
        scratch_shapes=[
            pltpu.VMEM((2 * NX, ROWS, W + TAG), bf16),
            pltpu.VMEM((2 * NX, ROWS, W), bf16),
            pltpu.VMEM((TAG, W), bf16),
            pltpu.VMEM((4, CHUNKS, CHUNK, W), bf16),
            pltpu.VMEM((4, BLOCK, TAG), bf16),
            pltpu.VMEM((4, 2 * NX, ROWS, BLOCK), f32),
            pltpu.VMEM((4, 2 * NX, ROWS, BLOCK), f32),
            pltpu.VMEM((2, 4, ROWS, BLOCK), bf16),
            pltpu.VMEM((2 * NX, 4, ROWS, BLOCK), bf16),
            pltpu.VMEM((NZ, NY, OWN, WA), bf16),
            pltpu.VMEM((NY, NZ, OWN, WB), bf16),
            pltpu.VMEM((NZ, NY, OWN, WA), bf16),
            pltpu.VMEM((NY, NZ, OWN, WB), bf16),
            pltpu.VMEM((NY, OWN, WA), bf16),
            pltpu.VMEM((NZ, OWN, WB), bf16),
            pltpu.VMEM((NY, OWN, WA), bf16),
            pltpu.VMEM((NZ, OWN, WB), bf16),
            pltpu.VMEM((NX, 2, W), f32),
            pltpu.VMEM((NX, 2, W), f32),
            dma((2 * NX,)), dma((2 * NX,)),
            dma((2, 6)), dma((2, 6)),
            dma((4, 2 * NX)), dma((4, 2 * NX)),
            dma((2 * NX,)), dma((2 * NX,)),
            dma((4, 8)), dma((4, 8)),
            dma((NX,)), dma((NX,)),
        ],
        compiler_params=pltpu.CompilerParams(
            collective_id=0, has_side_effects=True, vmem_limit_bytes=58 * 1024 * 1024
        ),
        name="estep",
    )(cut, mine, 1.0 / noise, prior)
    return (out, evidence.reshape(ROWS))


def solution(mesh):
    in_specs = (
        P(("cls", "img"), None),
        P("cls", None),
        P(),
        P(),
        P(("cls", "img")),
        P(("cls", "img")),
    )
    out_specs = (P(("cls", "img"), None), P(("cls", "img")))
    return jax.shard_map(body, mesh=mesh, in_specs=in_specs, out_specs=out_specs, check_vma=False)
```

time: 187 us -> 139 us (0.74)
  the two profiles are of different devices: /device:TPU:64 before, /device:TPU:2 now
where the time goes in v1:
time: 139 us
  Pallas kernels  126 us (91%)
  other arithmetic  7.08 us (5%)
  local copies, waits for them, and re-layouts  5.33 us (4%)
    pallas_call x1, Pallas kernels, body(): pl.pallas_call(kernel, out_shape=(jax.ShapeDtypeStruct((2, F), f32), jax....  126 us
    mul x1, other arithmetic, body(): sum((jnp.where(place == n, class_logprior[n], 0.0) for n in range(CLASSES)))  3.16 us

profile of v1, /device:TPU:2, one launch (start us, length us, event | category | flops | bytes accessed | tf_op | source)
XLA Modules:
  0.0 139.1 jit_solution(15347822979844432926)
XLA Ops:
  0.7 0.8 or_convert_fusion
  1.4 1.2 pad.12
  2.6 0.0 copy-start
  2.7 0.1 copy.13
  2.7 1.0 maximum_bitcast_fusion.img_ref
  3.8 0.0 copy-start.1
  3.8 0.7 copy-done
  4.5 0.0 copy-start.2
  4.5 0.2 pad_dynamic-slice_fusion
  4.7 1.0 copy.10
  5.7 0.0 copy-done.1
  5.7 0.7 fusion.inv_ref
  6.5 0.0 copy-done.2
  6.5 0.6 fusion.2
  7.1 3.2 %add_multiply_fusion.prior_ref = f32[4,128]{1,0:T(4,128)} fusion(f32[]{:T(128)} %bitcast.5, f32[]{:T(128)} %bitcast.4, f32[]{:T(128)} %bitcast.3, f32[]{:T(128)} %bitcast.2, s32[4]{0:T(128)S(1)} %add_add_fusion), kind=kLoop, calls=%fused_computation.10 | loop fusion | flops 12288 | bytes 2080 | tf_op jit(solution)/shard_map/mul | solution.py:356
  10.3 126.0 %estep.1 = (f32[2,7200]{1,0:T(2,128)}, f32[56,1]{1,0:T(8,128)}) custom-call(bf16[4,56,2048]{2,1,0:T(8,128)(2,1)} %maximum_bitcast_fusion.img_ref, bf16[4,32,1920]{2,1,0:T(8,128)(2,1)} %bitcast.13, f32[32,1920]{1,0:T(8,128)} %fusion.inv_ref, f32[4,128]{1,0:T(4,128)} %add_multiply_fusion.prior_ref), custom_call_target="tpu_custom_call" | custom-call | tf_op jit(solution)/shard_map/estep/pallas_call | solution.py:358
  136.3 1.4 reduce
  137.6 1.4 %copy.15 = f32[2,7200]{1,0:T(2,128)} copy(f32[2,7200]{1,0:T(2,128)} %get-tuple-element.16) | data formatting | bytes 115200
  (4 shorter events, 0.0 us)
Async XLA Ops:
  2.6 1.8 %copy-start = (bf16[128,7200]{0,1:T(8,128)(2,1)S(1)}, bf16[128,7200]{0,1:T(8,128)(2,1)}, u32[]{:S(2)}) copy-start(bf16[128,7200]{0,1:T(8,128)(2,1)} %param.7) | copy-start | bytes 5529604
  3.8 2.0 %copy-start.1 = (f32[32,7200]{1,0:T(8,128)S(1)}, f32[32,7200]{1,0:T(8,128)}, u32[]{:S(2)}) copy-start(f32[32,7200]{1,0:T(8,128)} %param.8) | copy-start | bytes 2764804
  4.5 2.0 %copy-start.2 = (f32[4]{0:T(128)S(1)}, f32[4]{0:T(128)}, u32[]{:S(2)}) copy-start(f32[4]{0:T(128)} %param.9) | copy-start | bytes 52

commit v2 on v1

v2 whole, which is shorter than its diff:
```python
import jax
import jax.numpy as jnp
from jax import lax
from jax.experimental import pallas as pl
from jax.experimental.pallas import tpu as pltpu
from jax.sharding import PartitionSpec as P

NX, NY, NZ = 4, 8, 8
F = 7200
W = 1920
TAG = 128
ROWS = 56
ALL = 2 * NX * ROWS
BLOCK = 128
CHUNKS = 4
CHUNK = W // CHUNKS
LAST = F - (NX - 1) * W
WA = 1024
WB = W - WA
GROUPS = 32
CLASSES = 4
OWN = 8
NN = (((1,), (0,)), ((), ()))
TN = (((0,), (0,)), ((), ()))
f32 = jnp.float32
bf16 = jnp.bfloat16


def kernel(
    img_hbm, proj_hbm, noise_hbm, prior_ref, group_ref, offset_ref, out_ref, ev_ref,
    img_v, noise_v, img_ref, xin, white, inv3, pbuf, qbuf, sc_send, sc_recv, post_send, post_recv,
    sum_a, sum_b, r1a, r1b, mid_a, mid_b, r2a, r2b, fin_send, fin_recv,
    load, img_s, img_r, cross_s, cross_r, pair_s, pair_r, sc_s, sc_r, post_s, post_r,
    rs_s, rs_r, fin_s, fin_r,
):
    cls = lax.axis_index("cls")
    img = lax.axis_index("img")
    h, c = cls // 2, cls % 2
    lo, z, x = img // (NZ * NX), (img // NX) % NZ, img % NX
    y = 2 * h + lo
    turn = (0, 3 - 2 * lo, 1 + 2 * lo, 2)

    def device(y_, z_, x_, c_):
        return {"cls": (y_ // 2) * 2 + c_, "img": ((y_ % 2) * NZ + z_) * NX + x_}

    def group(dx, dc):
        return device(y, z, (x + dx) % NX, (c + dc) % 2)

    def along_y(d):
        return device((y + d) % NY, z, x, c)

    def along_z(d):
        return device(y, (z + d) % NZ, x, c)

    across = device((y + NY - 1 + 2 * lo) % NY, z, x, c)
    beside = device(y + 1 - 2 * lo, z, x, c)

    def copy(src, dst, send, recv, to):
        return pltpu.make_async_remote_copy(
            src_ref=src, dst_ref=dst, send_sem=send, recv_sem=recv,
            device_id=to, device_id_type=pl.DeviceIdType.MESH,
        )

    load_img = pltpu.make_async_copy(img_hbm, img_v, load.at[0])
    load_noise = pltpu.make_async_copy(noise_hbm, noise_v, load.at[1])

    def load_proj(i):
        start = pl.multiple_of(x * W, 8) + i * CHUNK
        return pltpu.make_async_copy(
            proj_hbm.at[pl.ds(start, CHUNK)], pbuf.at[0, i], load.at[2 + i]
        )

    load_img.start()
    for i in range(CHUNKS - 1):
        load_proj(i).start()

    @pl.when(x < NX - 1)
    def _():
        load_proj(CHUNKS - 1).start()

    load_noise.start()

    barrier = pltpu.get_barrier_semaphore()
    partners = [group(s // 2, s % 2) for s in range(1, 2 * NX)]
    partners += [along_y(d) for d in range(1, NY)] + [along_z(d) for d in range(1, NZ)]
    for to in partners:
        pl.semaphore_signal(barrier, inc=1, device_id=to, device_id_type=pl.DeviceIdType.MESH)

    tag = lax.broadcasted_iota(jnp.int32, (TAG, ROWS), 0)
    is_group = (tag < 96) & (tag % 32 == group_ref[...])
    is_offset = (tag >= 96) & (tag < 108) & (tag % 4 == offset_ref[...])
    tags = jnp.transpose(jnp.where(is_group | is_offset, 1.0, 0.0).astype(f32)).astype(bf16)
    load_img.wait()
    for k in range(NX):
        end = min(F, W * (k + 1))
        img_ref[k, :, : end - W * k] = img_v[:, W * k : end]
        if end - W * k < W:
            img_ref[k, :, end - W * k : W] = jnp.zeros((ROWS, W * (k + 1) - end), bf16)
        img_ref[k, :, W:] = tags
    for i in range(CHUNKS - 1):
        load_proj(i).wait()

    @pl.when(x < NX - 1)
    def _():
        load_proj(CHUNKS - 1).wait()

    @pl.when(x == NX - 1)
    def _():
        pbuf[0, CHUNKS - 1] = jnp.zeros((CHUNK, BLOCK), bf16)

    pl.semaphore_wait(barrier, len(partners))

    def to_across(m):
        mine = (m + 2 * (1 - lo)) % CHUNKS
        src, dst = (pbuf.at[0, mine], pbuf.at[1, mine])
        if m >= CHUNKS:
            src, dst = (pbuf.at[2, mine], pbuf.at[3, mine])
        return copy(src, dst, cross_s.at[m], cross_r.at[m], across)

    def from_across(m):
        chunk = (m + 2 * lo) % CHUNKS
        return pbuf.at[1 if m < CHUNKS else 3, chunk]

    def to_beside(m):
        dst = pbuf.at[2 if m < CHUNKS else 3, (m + 2 * lo) % CHUNKS]
        return copy(from_across(m), dst, pair_s.at[m], pair_r.at[m], beside)

    def crossed(m):
        ref = from_across(m)
        copy(ref, ref, cross_s.at[m], cross_r.at[m], across).wait_recv()
        to_beside(m).start()

    def paired(m):
        ref = pbuf.at[2 if m < CHUNKS else 3, (m + 2 * (1 - lo)) % CHUNKS]
        copy(ref, ref, pair_s.at[m], pair_r.at[m], beside).wait_recv()
        if m < 2:
            to_across(CHUNKS + m).start()

    def image(dx):
        return copy(
            img_ref.at[(x + dx) % NX], xin.at[2 * dx], img_s.at[2 * dx], img_r.at[2 * dx],
            group(dx, 0),
        )

    def to_sibling(dx):
        src = img_ref.at[x] if dx == 0 else xin.at[2 * dx]
        s = 2 * dx + 1
        return copy(src, xin.at[s], img_s.at[s], img_r.at[s], group(0, 1))

    for m in range(CHUNKS):
        to_across(m).start()
    for dx in (2, 1, 3):
        image(dx).start()
    to_sibling(0).start()

    xin[0] = img_ref[x]
    load_noise.wait()

    def pieces(inv, width):
        hi = inv.astype(bf16)
        rest = inv - hi.astype(f32)
        mid = rest.astype(bf16)
        low = (rest - mid.astype(f32)).astype(bf16)
        inv3[0:GROUPS, :width] = hi
        inv3[GROUPS : 2 * GROUPS, :width] = mid
        inv3[2 * GROUPS : 3 * GROUPS, :width] = low

    inv3[3 * GROUPS :] = jnp.zeros((TAG - 3 * GROUPS, W), bf16)

    @pl.when(x < NX - 1)
    def _():
        pieces(1.0 / noise_v[:, pl.ds(pl.multiple_of(x * W, 128), W)], W)

    @pl.when(x == NX - 1)
    def _():
        pieces(1.0 / noise_v[:, F - LAST :], LAST)
        inv3[: 3 * GROUPS, LAST:] = jnp.zeros((3 * GROUPS, W - LAST), bf16)

    row = lax.broadcasted_iota(jnp.int32, (TAG, BLOCK), 0)
    piece = jnp.where(row < 96, row // 32, jnp.minimum((row - 96) // 4, 3))

    def block_of(slot):
        return pbuf[slot].reshape(W, BLOCK)

    def columns(slot):
        p = block_of(slot).astype(f32)
        square = p * p
        s_hi = square.astype(bf16)
        s_lo = (square - s_hi.astype(f32)).astype(bf16)
        q = lax.dot_general(inv3[...], s_hi, NN, preferred_element_type=f32)
        q += lax.dot_general(inv3[...], s_lo, NN, preferred_element_type=f32)
        q = q[0:32] + q[32:64] + q[64:96]
        prior = jnp.zeros((TAG, BLOCK), f32)
        for o in range(CLASSES):
            log_prior = prior_ref[0, (h + turn[slot] + CLASSES - o) % CLASSES]
            prior = jnp.where(row % CLASSES == o, log_prior * (1.0 / NX), prior)
        value = jnp.where(row < 96, -0.5 * jnp.concatenate([q] * 4, axis=0), prior)
        v_hi = value.astype(bf16).astype(f32)
        v_mid = (value - v_hi).astype(bf16).astype(f32)
        v_lo = value - v_hi - v_mid
        both = jnp.where(piece == 2, v_lo, 0.0)
        both = jnp.where(piece == 1, v_mid, both)
        qbuf[slot] = jnp.where(piece == 0, v_hi, both).astype(bf16)

    def image_arrived(dx):
        image(dx).wait_recv()
        to_sibling(dx).start()

    def score_copy(slot, s):
        return copy(
            sc_send.at[slot, s], sc_recv.at[slot, s], sc_s.at[slot, s], sc_r.at[slot, s],
            group((NX - s // 2) % NX, s % 2),
        )

    def scores(slot):
        part = lax.dot_general(
            white[...].reshape(ALL, W), block_of(slot), NN, preferred_element_type=f32
        )
        part += lax.dot_general(
            xin[:, :, W:].reshape(ALL, TAG), qbuf[slot], NN, preferred_element_type=f32
        )
        sc_send[slot] = part.reshape(2 * NX, ROWS, BLOCK)
        for s in (4, 5, 2, 3, 6, 7, 1):
            score_copy(slot, s).start()

    def whiten(s):
        inverse = jnp.dot(xin[s, :, W:], inv3[...], preferred_element_type=f32)
        white[s] = (xin[s, :, :W].astype(f32) * inverse).astype(bf16)

    whiten(0)
    columns(0)
    crossed(0)
    crossed(1)
    paired(0)
    image_arrived(1)
    image_arrived(3)
    crossed(2)
    paired(1)
    image_arrived(2)
    crossed(3)
    for s in (2, 6, 4):
        whiten(s)
    columns(1)
    for s in (1, 3, 7, 5):
        to_sibling(s // 2).wait_recv()
        whiten(s)
    scores(0)
    scores(1)
    crossed(4)
    paired(2)
    paired(3)
    columns(2)
    scores(2)
    crossed(5)
    paired(4)
    paired(5)
    columns(3)
    scores(3)

    total = {}
    for slot in range(4):
        for s in range(1, 2 * NX):
            score_copy(slot, s).wait_recv()
        for dc in (0, 1):
            parts = [sc_send[slot, 0]] if dc == 0 else [sc_recv[slot, 1]]
            parts += [sc_recv[slot, 2 * dx + dc] for dx in range(1, NX)]
            total[slot, dc] = (parts[0] + parts[1]) + (parts[2] + parts[3])
    peak = None
    for value in total.values():
        peak = value if peak is None else jnp.maximum(peak, value)
    peak = jnp.max(peak, axis=1, keepdims=True)
    mass = None
    for value in total.values():
        term = jnp.exp(value - peak)
        mass = term if mass is None else mass + term
    evidence = peak + jnp.log(jnp.sum(mass, axis=1, keepdims=True))
    ev_ref[...] = jnp.transpose(jnp.broadcast_to(evidence, (ROWS, TAG)))[0:1, :]
    for (slot, dc), value in total.items():
        post_send[dc, slot] = jnp.exp(value - evidence).astype(bf16)

    def post_copy(s):
        return copy(
            post_send.at[s % 2], post_recv.at[s], post_s.at[s], post_r.at[s], group(s // 2, s % 2)
        )

    for s in (4, 5, 2, 3, 6, 7, 1):
        post_copy(s).start()
    post_recv[0] = post_send[0]
    for s in (1, 2, 3, 6, 7, 4, 5):
        post_copy(s).wait_recv()

    def weights(slot):
        return post_recv[:, slot].reshape(ALL, BLOCK)

    def rs(which, d, src, dst, to):
        return copy(src, dst, rs_s.at[which, d], rs_r.at[which, d], to)

    def first_b(d):
        return rs(0, d, sum_b.at[(lo + d) % NY], r1b.at[d], along_y(d))

    def first_a(d):
        return rs(1, d, sum_a.at[(z + d) % NZ], r1a.at[d], along_z(d))

    def second_b(d):
        return rs(2, d, mid_b.at[(z + d) % NZ], r2b.at[d], along_z(d))

    def second_a(d):
        return rs(3, d, mid_a.at[(lo + d) % NY], r2a.at[d], along_y(d))

    far_first = (4, 3, 5, 2, 6, 1, 7)
    near_first = (1, 7, 2, 6, 3, 5, 4)
    for slot in range(4):
        part = lax.dot_general(
            weights(slot), white[:, :, WA:].reshape(ALL, WB), TN, preferred_element_type=f32
        ).astype(bf16)
        for r in range(2 * NZ):
            sum_b[2 * turn[slot] + r // NZ, r % NZ] = part[OWN * r : OWN * (r + 1)]
    for d in far_first:
        first_b(d).start()
    for slot in range(4):
        part = lax.dot_general(
            weights(slot), white[:, :, :WA].reshape(ALL, WA), TN, preferred_element_type=f32
        ).astype(bf16)
        for r in range(2 * NZ):
            sum_a[r % NZ, 2 * turn[slot] + r // NZ] = part[OWN * r : OWN * (r + 1)]
    for d in far_first:
        first_a(d).start()

    for d in near_first:
        first_b(d).wait_recv()
    for q in range(NZ):
        acc = sum_b[lo, q].astype(f32)
        for d in range(1, NY):
            acc += r1b[d, q].astype(f32)
        mid_b[q] = acc.astype(bf16)
    for d in far_first:
        second_b(d).start()
    for d in near_first:
        first_a(d).wait_recv()
    for q in range(NY):
        acc = sum_a[z, q].astype(f32)
        for d in range(1, NZ):
            acc += r1a[d, q].astype(f32)
        mid_a[q] = acc.astype(bf16)
    for d in far_first:
        second_a(d).start()

    for d in near_first:
        second_b(d).wait_recv()
    acc_b = mid_b[z].astype(f32)
    for d in range(1, NZ):
        acc_b += r2b[d].astype(f32)
    for d in near_first:
        second_a(d).wait_recv()
    acc_a = mid_a[lo].astype(f32)
    for d in range(1, NY):
        acc_a += r2a[d].astype(f32)

    def fin(d):
        return copy(
            fin_send.at[(x + d) % NX], fin_recv.at[x], fin_s.at[d], fin_r.at[d], group(d, 0)
        )

    def fin_in(d):
        return copy(
            fin_send.at[x], fin_recv.at[(x + NX - d) % NX], fin_s.at[d], fin_r.at[d], group(d, 0)
        )

    for k in range(NX):
        fin_send[k, :, :WA] = acc_a[2 * k : 2 * k + 2]
        fin_send[k, :, WA:] = acc_b[2 * k : 2 * k + 2]
    for d in (2, 1, 3):
        fin(d).start()
    fin_recv[x] = fin_send[x]
    for d in (1, 3, 2):
        fin_in(d).wait_recv()
    for k in range(NX):
        end = min(F, W * (k + 1))
        out_ref[:, W * k : end] = fin_recv[k, :, : end - W * k]

    for m in range(6):
        to_across(m).wait_send()
        to_beside(m).wait_send()
    for dx in range(NX):
        if dx:
            image(dx).wait_send()
        to_sibling(dx).wait_send()
    for s in range(1, 2 * NX):
        for slot in range(4):
            score_copy(slot, s).wait_send()
        post_copy(s).wait_send()
    for d in range(1, NY):
        first_a(d).wait_send()
        first_b(d).wait_send()
        second_a(d).wait_send()
        second_b(d).wait_send()
    for d in range(1, NX):
        fin(d).wait_send()


def body(images, projections, noise_power, class_logprior, groups, offsets):
    dma = pltpu.SemaphoreType.DMA
    anywhere = pl.BlockSpec(memory_space=pl.ANY)
    vmem = pl.BlockSpec(memory_space=pltpu.VMEM)
    out, evidence = pl.pallas_call(
        kernel,
        out_shape=(
            jax.ShapeDtypeStruct((2, F), f32),
            jax.ShapeDtypeStruct((1, ROWS), f32),
        ),
        in_specs=[anywhere] * 3 + [pl.BlockSpec(memory_space=pltpu.SMEM), vmem, vmem],
        out_specs=(vmem, vmem),
        scratch_shapes=[
            pltpu.VMEM((ROWS, F), bf16),
            pltpu.VMEM((GROUPS, F), f32),
            pltpu.VMEM((NX, ROWS, W + TAG), bf16),
            pltpu.VMEM((2 * NX, ROWS, W + TAG), bf16),
            pltpu.VMEM((2 * NX, ROWS, W), bf16),
            pltpu.VMEM((TAG, W), bf16),
            pltpu.VMEM((4, CHUNKS, CHUNK, BLOCK), bf16),
            pltpu.VMEM((4, TAG, BLOCK), bf16),
            pltpu.VMEM((4, 2 * NX, ROWS, BLOCK), f32),
            pltpu.VMEM((4, 2 * NX, ROWS, BLOCK), f32),
            pltpu.VMEM((2, 4, ROWS, BLOCK), bf16),
            pltpu.VMEM((2 * NX, 4, ROWS, BLOCK), bf16),
            pltpu.VMEM((NZ, NY, OWN, WA), bf16),
            pltpu.VMEM((NY, NZ, OWN, WB), bf16),
            pltpu.VMEM((NZ, NY, OWN, WA), bf16),
            pltpu.VMEM((NY, NZ, OWN, WB), bf16),
            pltpu.VMEM((NY, OWN, WA), bf16),
            pltpu.VMEM((NZ, OWN, WB), bf16),
            pltpu.VMEM((NY, OWN, WA), bf16),
            pltpu.VMEM((NZ, OWN, WB), bf16),
            pltpu.VMEM((NX, 2, W), f32),
            pltpu.VMEM((NX, 2, W), f32),
            dma((2 + CHUNKS,)),
            dma((2 * NX,)), dma((2 * NX,)),
            dma((6,)), dma((6,)),
            dma((6,)), dma((6,)),
            dma((4, 2 * NX)), dma((4, 2 * NX)),
            dma((2 * NX,)), dma((2 * NX,)),
            dma((4, 8)), dma((4, 8)),
            dma((NX,)), dma((NX,)),
        ],
        compiler_params=pltpu.CompilerParams(
            collective_id=0, has_side_effects=True, vmem_limit_bytes=58 * 1024 * 1024
        ),
        name="estep",
    )(
        images, projections.T, noise_power, class_logprior.reshape(1, CLASSES),
        groups.reshape(1, ROWS), offsets.reshape(1, ROWS),
    )
    return (out, evidence.reshape(ROWS))


def solution(mesh):
    in_specs = (
        P(("cls", "img"), None),
        P("cls", None),
        P(),
        P(),
        P(("cls", "img")),
        P(("cls", "img")),
    )
    out_specs = (P(("cls", "img"), None), P(("cls", "img")))
    return jax.shard_map(body, mesh=mesh, in_specs=in_specs, out_specs=out_specs, check_vma=False)
```

time: 139 us -> 94.3 us (0.68)
  the two profiles are of different devices: /device:TPU:2 before, /device:TPU:1 now
where the time goes in v2:
time: 94.3 us; the launch traced here: 94 us
  Pallas kernels  90.8 us (96%)
  local copies, waits for them, and re-layouts  2.57 us (3%)
    pallas_call x1, Pallas kernels, body(): pl.pallas_call(kernel, out_shape=(jax.ShapeDtypeStruct((2, F), f32), jax....  90.8 us
    unnamed x2, local copies, waits for them, and re-layouts  2.57 us

profile of v2, /device:TPU:1, one launch (start us, length us, event | category | flops | bytes accessed | tf_op | source)
XLA Modules:
  0.0 94.0 jit_solution(4581161661214182332)
XLA Ops:
  0.6 90.8 %estep.1 = (f32[2,7200]{1,0:T(2,128)}, f32[1,56]{1,0:T(1,128)}) custom-call(bf16[56,7200]{1,0:T(8,128)(2,1)} %img_hbm.1, bf16[7200,128]{1,0:T(8,128)(2,1)} %bitcast.5, f32[32,7200]{1,0:T(8,128)} %noise_hbm.1, f32[1,4]{1,0:T(1,128)} %bitcast.6, s32[1,56]{1,0:T(1,128)} %bitcast.7, s32[1,56]{1,0:T(1,128)} %bitcast.8), custom_call_target="tpu_custom_call" | custom-call | tf_op jit(solution)/shard_map/estep/pallas_call | solution.py:405
  91.5 1.4 %copy.10 = f32[2,7200]{1,0:T(2,128)} copy(f32[2,7200]{1,0:T(2,128)} %get-tuple-element.8) | data formatting | bytes 115200
  92.9 1.1 %copy.11 = f32[56]{0:T(128)} copy(f32[56]{0:T(128)} %bitcast.9) | data formatting | bytes 448

commit v3 on v2

--- a/solution.py
+++ b/solution.py
@@ -13,7 +13,11 @@
 ALL = 2 * NX * ROWS
 BLOCK = 128
 CHUNKS = 4
-CHUNK = W // CHUNKS
+PARTS = 2 * CHUNKS
+CHUNK = W // PARTS
+WHOLE = F // CHUNK - (NX - 1) * PARTS
+STEPS = (0, 1, 3, 2)
+EARLY = 6
 LAST = F - (NX - 1) * W
 WA = 1024
 WB = W - WA
@@ -26,11 +30,18 @@
 bf16 = jnp.bfloat16
 
 
+def finish(fin_ref, ev_ref, out_ref, evidence_ref):
+    for k in range(NX):
+        end = min(F, W * (k + 1))
+        out_ref[:, W * k : end] = fin_ref[k, :, : end - W * k]
+    evidence_ref[...] = ev_ref[...]
+
+
 def kernel(
     img_hbm, proj_hbm, noise_hbm, prior_ref, group_ref, offset_ref, out_ref, ev_ref,
     img_v, noise_v, img_ref, xin, white, inv3, pbuf, qbuf, sc_send, sc_recv, post_send, post_recv,
     sum_a, sum_b, r1a, r1b, mid_a, mid_b, r2a, r2b, fin_send, fin_recv,
-    load, img_s, img_r, cross_s, cross_r, pair_s, pair_r, sc_s, sc_r, post_s, post_r,
+    load, img_s, img_r, cross_s, cross_r, pair_s, pair_r, side_s, side_r, sc_s, sc_r, post_s, post_r,
     rs_s, rs_r, fin_s, fin_r,
 ):
     cls = lax.axis_index("cls")
@@ -39,6 +50,7 @@
     lo, z, x = img // (NZ * NX), (img // NX) % NZ, img % NX
     y = 2 * h + lo
     turn = (0, 3 - 2 * lo, 1 + 2 * lo, 2)
+    half = z % 2
 
     def device(y_, z_, x_, c_):
         return {"cls": (y_ // 2) * 2 + c_, "img": ((y_ % 2) * NZ + z_) * NX + x_}
@@ -64,19 +76,19 @@
     load_img = pltpu.make_async_copy(img_hbm, img_v, load.at[0])
     load_noise = pltpu.make_async_copy(noise_hbm, noise_v, load.at[1])
 
-    def load_proj(i):
-        start = pl.multiple_of(x * W, 8) + i * CHUNK
-        return pltpu.make_async_copy(
-            proj_hbm.at[pl.ds(start, CHUNK)], pbuf.at[0, i], load.at[2 + i]
-        )
-
+    load_proj = pltpu.make_async_copy(
+        proj_hbm.at[pl.ds(x * PARTS, WHOLE)], pbuf.at[0, pl.ds(0, WHOLE)], load.at[2]
+    )
+    load_rest = pltpu.make_async_copy(
+        proj_hbm.at[pl.ds((x % (NX - 1)) * PARTS + WHOLE, PARTS - WHOLE)],
+        pbuf.at[0, pl.ds(WHOLE, PARTS - WHOLE)], load.at[3],
+    )
     load_img.start()
-    for i in range(CHUNKS - 1):
-        load_proj(i).start()
+    load_proj.start()
 
     @pl.when(x < NX - 1)
     def _():
-        load_proj(CHUNKS - 1).start()
+        load_rest.start()
 
     load_noise.start()
 
@@ -97,60 +109,77 @@
         if end - W * k < W:
             img_ref[k, :, end - W * k : W] = jnp.zeros((ROWS, W * (k + 1) - end), bf16)
         img_ref[k, :, W:] = tags
-    for i in range(CHUNKS - 1):
-        load_proj(i).wait()
+    load_proj.wait()
 
     @pl.when(x < NX - 1)
     def _():
-        load_proj(CHUNKS - 1).wait()
+        load_rest.wait()
 
     @pl.when(x == NX - 1)
     def _():
-        pbuf[0, CHUNKS - 1] = jnp.zeros((CHUNK, BLOCK), bf16)
+        pbuf[0, WHOLE:] = jnp.zeros((PARTS - WHOLE, CHUNK, BLOCK), bf16)
 
     pl.semaphore_wait(barrier, len(partners))
 
+    def turned(m, low):
+        return (m + 2 * low) % CHUNKS
+
     def to_across(m):
-        mine = (m + 2 * (1 - lo)) % CHUNKS
+        mine = half * CHUNKS + turned(m, 1 - lo)
         src, dst = (pbuf.at[0, mine], pbuf.at[1, mine])
         if m >= CHUNKS:
             src, dst = (pbuf.at[2, mine], pbuf.at[3, mine])
         return copy(src, dst, cross_s.at[m], cross_r.at[m], across)
 
     def from_across(m):
-        chunk = (m + 2 * lo) % CHUNKS
-        return pbuf.at[1 if m < CHUNKS else 3, chunk]
+        return pbuf.at[1 if m < CHUNKS else 3, half * CHUNKS + turned(m, lo)]
 
     def to_beside(m):
-        dst = pbuf.at[2 if m < CHUNKS else 3, (m + 2 * lo) % CHUNKS]
+        dst = pbuf.at[2 if m < CHUNKS else 3, half * CHUNKS + turned(m, lo)]
         return copy(from_across(m), dst, pair_s.at[m], pair_r.at[m], beside)
+
+    def from_beside(m):
+        return pbuf.at[2 if m < CHUNKS else 3, half * CHUNKS + turned(m, 1 - lo)]
+
+    def to_side(way, m):
+        ref = from_across(m) if way == 0 else from_beside(m)
+        up = 1 - 2 * (turned(m, lo if way == 0 else 1 - lo) // 2)
+        to = device(y, (z + NZ + up) % NZ, x, c)
+        return copy(ref, ref, side_s.at[way, m], side_r.at[way, m], to)
+
+    def sided(way, m):
+        chunk = (1 - half) * CHUNKS + turned(m, lo if way == 0 else 1 - lo)
+        ref = pbuf.at[(1 + way) if m < CHUNKS else 3, chunk]
+        copy(ref, ref, side_s.at[way, m], side_r.at[way, m], along_z(1)).wait_recv()
 
     def crossed(m):
         ref = from_across(m)
         copy(ref, ref, cross_s.at[m], cross_r.at[m], across).wait_recv()
         to_beside(m).start()
+        to_side(0, m).start()
 
     def paired(m):
-        ref = pbuf.at[2 if m < CHUNKS else 3, (m + 2 * (1 - lo)) % CHUNKS]
+        ref = from_beside(m)
         copy(ref, ref, pair_s.at[m], pair_r.at[m], beside).wait_recv()
         if m < 2:
             to_across(CHUNKS + m).start()
-
-    def image(dx):
+        to_side(1, m).start()
+
+    def image(p):
         return copy(
-            img_ref.at[(x + dx) % NX], xin.at[2 * dx], img_s.at[2 * dx], img_r.at[2 * dx],
-            group(dx, 0),
-        )
-
-    def to_sibling(dx):
-        src = img_ref.at[x] if dx == 0 else xin.at[2 * dx]
-        s = 2 * dx + 1
+            img_ref.at[(x + STEPS[p]) % NX], xin.at[2 * p], img_s.at[2 * p], img_r.at[2 * p],
+            group(STEPS[p], 0),
+        )
+
+    def to_sibling(p):
+        src = img_ref.at[x] if p == 0 else xin.at[2 * p]
+        s = 2 * p + 1
         return copy(src, xin.at[s], img_s.at[s], img_r.at[s], group(0, 1))
 
     for m in range(CHUNKS):
         to_across(m).start()
-    for dx in (2, 1, 3):
-        image(dx).start()
+    for p in (1, 2, 3):
+        image(p).start()
     to_sibling(0).start()
 
     xin[0] = img_ref[x]
@@ -202,26 +231,28 @@
         both = jnp.where(piece == 1, v_mid, both)
         qbuf[slot] = jnp.where(piece == 0, v_hi, both).astype(bf16)
 
-    def image_arrived(dx):
-        image(dx).wait_recv()
-        to_sibling(dx).start()
+    def image_arrived(p):
+        image(p).wait_recv()
+        to_sibling(p).start()
 
     def score_copy(slot, s):
         return copy(
             sc_send.at[slot, s], sc_recv.at[slot, s], sc_s.at[slot, s], sc_r.at[slot, s],
-            group((NX - s // 2) % NX, s % 2),
-        )
-
-    def scores(slot):
+            group((NX - STEPS[s // 2]) % NX, s % 2),
+        )
+
+    def scores(slot, first, last):
+        rows = (last - first) * ROWS
         part = lax.dot_general(
-            white[...].reshape(ALL, W), block_of(slot), NN, preferred_element_type=f32
+            white[first:last].reshape(rows, W), block_of(slot), NN, preferred_element_type=f32
         )
         part += lax.dot_general(
-            xin[:, :, W:].reshape(ALL, TAG), qbuf[slot], NN, preferred_element_type=f32
-        )
-        sc_send[slot] = part.reshape(2 * NX, ROWS, BLOCK)
-        for s in (4, 5, 2, 3, 6, 7, 1):
-            score_copy(slot, s).start()
+            xin[first:last, :, W:].reshape(rows, TAG), qbuf[slot], NN, preferred_element_type=f32
+        )
+        sc_send[slot, first:last] = part.reshape(last - first, ROWS, BLOCK)
+        for s in (6, 7, 2, 4, 3, 5, 1):
+            if first <= s < last:
+                score_copy(slot, s).start()
 
     def whiten(s):
         inverse = jnp.dot(xin[s, :, W:], inv3[...], preferred_element_type=f32)
@@ -231,31 +262,43 @@
     columns(0)
     crossed(0)
     crossed(1)
+    crossed(2)
     paired(0)
+    crossed(3)
+    paired(1)
     image_arrived(1)
-    image_arrived(3)
-    crossed(2)
-    paired(1)
     image_arrived(2)
-    crossed(3)
-    for s in (2, 6, 4):
-        whiten(s)
-    columns(1)
-    for s in (1, 3, 7, 5):
+    whiten(2)
+    whiten(4)
+    paired(2)
+    crossed(4)
+    for s in (1, 3, 5):
         to_sibling(s // 2).wait_recv()
         whiten(s)
-    scores(0)
-    scores(1)
-    crossed(4)
-    paired(2)
     paired(3)
+    scores(0, 0, EARLY)
+    crossed(5)
+    for m in range(CHUNKS):
+        sided(0, m)
+    columns(1)
+    scores(1, 0, EARLY)
+    paired(4)
+    image_arrived(3)
+    whiten(6)
+    for m in range(CHUNKS):
+        sided(1, m)
     columns(2)
-    scores(2)
-    crossed(5)
-    paired(4)
     paired(5)
+    to_sibling(3).wait_recv()
+    whiten(7)
+    scores(0, EARLY, 2 * NX)
+    scores(1, EARLY, 2 * NX)
+    scores(2, 0, 2 * NX)
+    for m in (CHUNKS, CHUNKS + 1):
+        sided(0, m)
+        sided(1, m)
     columns(3)
-    scores(3)
+    scores(3, 0, 2 * NX)
 
     total = {}
     for slot in range(4):
@@ -280,13 +323,14 @@
 
     def post_copy(s):
         return copy(
-            post_send.at[s % 2], post_recv.at[s], post_s.at[s], post_r.at[s], group(s // 2, s % 2)
-        )
-
-    for s in (4, 5, 2, 3, 6, 7, 1):
+            post_send.at[s % 2], post_recv.at[s], post_s.at[s], post_r.at[s],
+            group(STEPS[s // 2], s % 2),
+        )
+
+    for s in (6, 7, 2, 4, 3, 5, 1):
         post_copy(s).start()
     post_recv[0] = post_send[0]
-    for s in (1, 2, 3, 6, 7, 4, 5):
+    for s in (1, 2, 4, 3, 5, 6, 7):
         post_copy(s).wait_recv()
 
     def weights(slot):
@@ -374,17 +418,17 @@
     fin_recv[x] = fin_send[x]
     for d in (1, 3, 2):
         fin_in(d).wait_recv()
-    for k in range(NX):
-        end = min(F, W * (k + 1))
-        out_ref[:, W * k : end] = fin_recv[k, :, : end - W * k]
+    out_ref[...] = fin_recv[...]
 
     for m in range(6):
         to_across(m).wait_send()
         to_beside(m).wait_send()
-    for dx in range(NX):
-        if dx:
-            image(dx).wait_send()
-        to_sibling(dx).wait_send()
+        to_side(0, m).wait_send()
+        to_side(1, m).wait_send()
+    for p in range(NX):
+        if p:
+            image(p).wait_send()
+        to_sibling(p).wait_send()
     for s in range(1, 2 * NX):
         for slot in range(4):
             score_copy(slot, s).wait_send()
@@ -405,7 +449,7 @@
     out, evidence = pl.pallas_call(
         kernel,
         out_shape=(
-            jax.ShapeDtypeStruct((2, F), f32),
+            jax.ShapeDtypeStruct((NX, 2, W), f32),
             jax.ShapeDtypeStruct((1, ROWS), f32),
         ),
         in_specs=[anywhere] * 3 + [pl.BlockSpec(memory_space=pltpu.SMEM), vmem, vmem],
@@ -417,7 +461,7 @@
             pltpu.VMEM((2 * NX, ROWS, W + TAG), bf16),
             pltpu.VMEM((2 * NX, ROWS, W), bf16),
             pltpu.VMEM((TAG, W), bf16),
-            pltpu.VMEM((4, CHUNKS, CHUNK, BLOCK), bf16),
+            pltpu.VMEM((4, PARTS, CHUNK, BLOCK), bf16),
             pltpu.VMEM((4, TAG, BLOCK), bf16),
             pltpu.VMEM((4, 2 * NX, ROWS, BLOCK), f32),
             pltpu.VMEM((4, 2 * NX, ROWS, BLOCK), f32),
@@ -433,10 +477,11 @@
             pltpu.VMEM((NZ, OWN, WB), bf16),
             pltpu.VMEM((NX, 2, W), f32),
             pltpu.VMEM((NX, 2, W), f32),
-            dma((2 + CHUNKS,)),
+            dma((4,)),
             dma((2 * NX,)), dma((2 * NX,)),
             dma((6,)), dma((6,)),
             dma((6,)), dma((6,)),
+            dma((2, 6)), dma((2, 6)),
             dma((4, 2 * NX)), dma((4, 2 * NX)),
             dma((2 * NX,)), dma((2 * NX,)),
             dma((4, 8)), dma((4, 8)),
@@ -447,9 +492,19 @@
         ),
         name="estep",
     )(
-        images, projections.T, noise_power, class_logprior.reshape(1, CLASSES),
+        images, projections.T.reshape(F // CHUNK, CHUNK, BLOCK), noise_power, class_logprior.reshape(1, CLASSES),
         groups.reshape(1, ROWS), offsets.reshape(1, ROWS),
     )
+    out, evidence = pl.pallas_call(
+        finish,
+        out_shape=(
+            jax.ShapeDtypeStruct((2, F), f32),
+            jax.ShapeDtypeStruct((1, ROWS), f32),
+        ),
+        in_specs=[vmem, vmem],
+        out_specs=(vmem, vmem),
+        name="finish",
+    )(out, evidence)
     return (out, evidence.reshape(ROWS))
 
 

time: 94.3 us -> 90.4 us (0.959)
  the two profiles are of different devices: /device:TPU:1 before, /device:TPU:8 now
where the time goes in v3:
time: 90.4 us; the launch traced here: 90.2 us
  Pallas kernels  89.6 us (99%)
    pallas_call x1, Pallas kernels, body(): pl.pallas_call(kernel, out_shape=(jax.ShapeDtypeStruct((NX, 2, W), f32),...  88.1 us

profile of v3, /device:TPU:8, one launch (start us, length us, event | category | flops | bytes accessed | tf_op | source)
XLA Modules:
  0.0 90.2 jit_solution(12903350148890831712)
XLA Ops:
  0.6 88.1 %estep.1 = (f32[4,2,1920]{2,1,0:T(2,128)}, f32[1,56]{1,0:T(1,128)}) custom-call(bf16[56,7200]{1,0:T(8,128)(2,1)} %img_hbm.1, bf16[30,240,128]{2,1,0:T(8,128)(2,1)} %bitcast.7, f32[32,7200]{1,0:T(8,128)} %noise_hbm.1, f32[1,4]{1,0:T(1,128)} %bitcast.8, s32[1,56]{1,0:T(1,128)} %bitcast.9, s32[1,56]{1,0:T(1,128)} %bitcast.10), custom_call_target="tpu_custom_call" | custom-call | tf_op jit(solution)/shard_map/estep/pallas_call | solution.py:449
  88.8 1.5 %finish.1 = (f32[2,7200]{1,0:T(2,128)}, f32[1,56]{1,0:T(1,128)}) custom-call(f32[4,2,1920]{2,1,0:T(2,128)} %get-tuple-element.6.fin_ref, f32[1,56]{1,0:T(1,128)} %get-tuple-element.7.ev_ref), custom_call_target="tpu_custom_call" | custom-call | tf_op jit(solution)/shard_map/finish/pallas_call | solution.py:498

commit v4 on v3

--- a/solution.py
+++ b/solution.py
@@ -24,8 +24,11 @@
 GROUPS = 32
 CLASSES = 4
 OWN = 8
+STREAMS = (
+    ("z", 1, 0, 256), ("z", -1, 256, 256), ("y", 1, 1024, 256), ("y", -1, 1280, 256),
+    ("z", 1, 512, 256), ("z", -1, 768, 256), ("y", 1, 1536, 256), ("y", -1, 1792, 128),
+)
 NN = (((1,), (0,)), ((), ()))
-TN = (((0,), (0,)), ((), ()))
 f32 = jnp.float32
 bf16 = jnp.bfloat16
 
@@ -40,9 +43,9 @@
 def kernel(
     img_hbm, proj_hbm, noise_hbm, prior_ref, group_ref, offset_ref, out_ref, ev_ref,
     img_v, noise_v, img_ref, xin, white, inv3, pbuf, qbuf, sc_send, sc_recv, post_send, post_recv,
-    sum_a, sum_b, r1a, r1b, mid_a, mid_b, r2a, r2b, fin_send, fin_recv,
+    wt, parts, in1, mid1, in2, mid2, in3, own, got,
     load, img_s, img_r, cross_s, cross_r, pair_s, pair_r, side_s, side_r, sc_s, sc_r, post_s, post_r,
-    rs_s, rs_r, fin_s, fin_r,
+    st_s, st_r, own_s, own_r,
 ):
     cls = lax.axis_index("cls")
     img = lax.axis_index("img")
@@ -94,7 +97,11 @@
 
     barrier = pltpu.get_barrier_semaphore()
     partners = [group(s // 2, s % 2) for s in range(1, 2 * NX)]
-    partners += [along_y(d) for d in range(1, NY)] + [along_z(d) for d in range(1, NZ)]
+    partners += [along_y(1), along_y(NY - 1), along_z(1), along_z(NZ - 1)]
+    for d in (2, 4, 6):
+        for e in range(NX):
+            partners += [device((y + d) % NY, z, (x + e) % NX, c)]
+            partners += [device(y, (z + d) % NZ, (x + e) % NX, c)]
     for to in partners:
         pl.semaphore_signal(barrier, inc=1, device_id=to, device_id_type=pl.DeviceIdType.MESH)
 
@@ -305,9 +312,9 @@
         for s in range(1, 2 * NX):
             score_copy(slot, s).wait_recv()
         for dc in (0, 1):
-            parts = [sc_send[slot, 0]] if dc == 0 else [sc_recv[slot, 1]]
-            parts += [sc_recv[slot, 2 * dx + dc] for dx in range(1, NX)]
-            total[slot, dc] = (parts[0] + parts[1]) + (parts[2] + parts[3])
+            terms = [sc_send[slot, 0]] if dc == 0 else [sc_recv[slot, 1]]
+            terms += [sc_recv[slot, 2 * dx + dc] for dx in range(1, NX)]
+            total[slot, dc] = (terms[0] + terms[1]) + (terms[2] + terms[3])
     peak = None
     for value in total.values():
         peak = value if peak is None else jnp.maximum(peak, value)
@@ -333,92 +340,107 @@
     for s in (1, 2, 4, 3, 5, 6, 7):
         post_copy(s).wait_recv()
 
-    def weights(slot):
-        return post_recv[:, slot].reshape(ALL, BLOCK)
-
-    def rs(which, d, src, dst, to):
-        return copy(src, dst, rs_s.at[which, d], rs_r.at[which, d], to)
-
-    def first_b(d):
-        return rs(0, d, sum_b.at[(lo + d) % NY], r1b.at[d], along_y(d))
-
-    def first_a(d):
-        return rs(1, d, sum_a.at[(z + d) % NZ], r1a.at[d], along_z(d))
-
-    def second_b(d):
-        return rs(2, d, mid_b.at[(z + d) % NZ], r2b.at[d], along_z(d))
-
-    def second_a(d):
-        return rs(3, d, mid_a.at[(lo + d) % NY], r2a.at[d], along_y(d))
-
-    far_first = (4, 3, 5, 2, 6, 1, 7)
-    near_first = (1, 7, 2, 6, 3, 5, 4)
     for slot in range(4):
-        part = lax.dot_general(
-            weights(slot), white[:, :, WA:].reshape(ALL, WB), TN, preferred_element_type=f32
+        wt[BLOCK * slot : BLOCK * (slot + 1)] = jnp.transpose(post_recv[:, slot].reshape(ALL, BLOCK))
+
+    place = {"z": z, "y": y}
+    other = {"z": "y", "y": "z"}
+
+    def along(axis, d):
+        at = (place[axis] + d + 8) % 8
+        return device(y, at, x, c) if axis == "z" else device(at, z, x, c)
+
+    def near(axis, side):
+        return along(axis, side * (1 - 2 * (place[axis] % 2)))
+
+    def stage1(i):
+        axis, side = STREAMS[i][:2]
+        return copy(
+            parts[i].at[1 - place[axis] % 2], in1[i], st_s.at[0, i], st_r.at[0, i], near(axis, side)
+        )
+
+    def stage2(i):
+        axis, side = STREAMS[i][:2]
+        return copy(
+            mid1[i].at[1 - place[other[axis]] % 2], in2[i], st_s.at[1, i], st_r.at[1, i],
+            near(other[axis], side),
+        )
+
+    def stage3(i, d):
+        axis = STREAMS[i][0]
+        return copy(
+            mid2[i].at[(place[axis] // 2 + d) % 4], in3[i].at[d - 1], st_s.at[1 + d, i],
+            st_r.at[1 + d, i], along(axis, 2 * d),
+        )
+
+    def last(axis, d, e):
+        n = "zy".index(axis)
+        at = (place[other[axis]] + 2 * d) % 8
+        to = device(at, z, (x + e) % NX, c) if axis == "z" else device(y, at, (x + e) % NX, c)
+        return copy(
+            own[n].at[(place[other[axis]] // 2 + d) % 4, (x + e) % NX], got[n].at[d, x],
+            own_s.at[n, 4 * d + e], own_r.at[n, 4 * d + e], to,
+        )
+
+    def last_in(axis, d, e):
+        n = "zy".index(axis)
+        ref = got[n].at[d, (x + NX - e) % NX]
+        return copy(ref, ref, own_s.at[n, 4 * d + e], own_r.at[n, 4 * d + e], group(1, 0))
+
+    order = range(len(STREAMS))
+    for i in order:
+        axis, _, col, width = STREAMS[i]
+        part = jnp.dot(
+            wt[...], white[:, :, col : col + width].reshape(ALL, width), preferred_element_type=f32
         ).astype(bf16)
-        for r in range(2 * NZ):
-            sum_b[2 * turn[slot] + r // NZ, r % NZ] = part[OWN * r : OWN * (r + 1)]
-    for d in far_first:
-        first_b(d).start()
-    for slot in range(4):
-        part = lax.dot_general(
-            weights(slot), white[:, :, :WA].reshape(ALL, WA), TN, preferred_element_type=f32
-        ).astype(bf16)
-        for r in range(2 * NZ):
-            sum_a[r % NZ, 2 * turn[slot] + r // NZ] = part[OWN * r : OWN * (r + 1)]
-    for d in far_first:
-        first_a(d).start()
-
-    for d in near_first:
-        first_b(d).wait_recv()
-    for q in range(NZ):
-        acc = sum_b[lo, q].astype(f32)
-        for d in range(1, NY):
-            acc += r1b[d, q].astype(f32)
-        mid_b[q] = acc.astype(bf16)
-    for d in far_first:
-        second_b(d).start()
-    for d in near_first:
-        first_a(d).wait_recv()
-    for q in range(NY):
-        acc = sum_a[z, q].astype(f32)
-        for d in range(1, NZ):
-            acc += r1a[d, q].astype(f32)
-        mid_a[q] = acc.astype(bf16)
-    for d in far_first:
-        second_a(d).start()
-
-    for d in near_first:
-        second_b(d).wait_recv()
-    acc_b = mid_b[z].astype(f32)
-    for d in range(1, NZ):
-        acc_b += r2b[d].astype(f32)
-    for d in near_first:
-        second_a(d).wait_recv()
-    acc_a = mid_a[lo].astype(f32)
-    for d in range(1, NY):
-        acc_a += r2a[d].astype(f32)
-
-    def fin(d):
-        return copy(
-            fin_send.at[(x + d) % NX], fin_recv.at[x], fin_s.at[d], fin_r.at[d], group(d, 0)
-        )
-
-    def fin_in(d):
-        return copy(
-            fin_send.at[x], fin_recv.at[(x + NX - d) % NX], fin_s.at[d], fin_r.at[d], group(d, 0)
-        )
-
-    for k in range(NX):
-        fin_send[k, :, :WA] = acc_a[2 * k : 2 * k + 2]
-        fin_send[k, :, WA:] = acc_b[2 * k : 2 * k + 2]
-    for d in (2, 1, 3):
-        fin(d).start()
-    fin_recv[x] = fin_send[x]
-    for d in (1, 3, 2):
-        fin_in(d).wait_recv()
-    out_ref[...] = fin_recv[...]
+        for slot in range(4):
+            y_half = (h + turn[slot]) % 4
+            for r in range(2 * NZ):
+                low, z_ = r // NZ, r % NZ
+                at = BLOCK * slot + OWN * r
+                if axis == "z":
+                    parts[i][z_ % 2, low, z_ // 2, y_half] = part[at : at + OWN]
+                else:
+                    parts[i][low, z_ % 2, y_half, z_ // 2] = part[at : at + OWN]
+        stage1(i).start()
+    for i in order:
+        axis = STREAMS[i][0]
+        stage1(i).wait_recv()
+        total = parts[i][place[axis] % 2].astype(f32) + in1[i][...].astype(f32)
+        mid1[i][...] = total.astype(bf16)
+        stage2(i).start()
+    for i in order:
+        axis = STREAMS[i][0]
+        stage2(i).wait_recv()
+        total = mid1[i][place[other[axis]] % 2].astype(f32) + in2[i][...].astype(f32)
+        mid2[i][...] = total.astype(bf16)
+        for d in (2, 1, 3):
+            stage3(i, d).start()
+    far_first = [(d, e) for d in (2, 1, 3, 0) for e in (2, 1, 3, 0) if d or e]
+    for axis in "zy":
+        n = "zy".index(axis)
+        for i in order:
+            if STREAMS[i][0] != axis:
+                continue
+            _, _, col, width = STREAMS[i]
+            col -= WA * n
+            acc = mid2[i][place[axis] // 2].astype(f32)
+            for d in (1, 3, 2):
+                stage3(i, d).wait_recv()
+                acc += in3[i][d - 1].astype(f32)
+            for k in range(NX):
+                own[n][:, k, :, col : col + width] = acc[:, 2 * k : 2 * k + 2].astype(bf16)
+        for d, e in far_first:
+            last(axis, d, e).start()
+        got[n][0, x] = own[n][place[other[axis]] // 2, x]
+    for axis in "zy":
+        n = "zy".index(axis)
+        for d, e in reversed(far_first):
+            last_in(axis, d, e).wait_recv()
+        acc = got[n][0].astype(f32)
+        for d in range(1, 4):
+            acc += got[n][d].astype(f32)
+        out_ref[:, :, WA * n : WA * n + (WA, WB)[n]] = acc
 
     for m in range(6):
         to_across(m).wait_send()
@@ -433,13 +455,14 @@
         for slot in range(4):
             score_copy(slot, s).wait_send()
         post_copy(s).wait_send()
-    for d in range(1, NY):
-        first_a(d).wait_send()
-        first_b(d).wait_send()
-        second_a(d).wait_send()
-        second_b(d).wait_send()
-    for d in range(1, NX):
-        fin(d).wait_send()
+    for i in order:
+        stage1(i).wait_send()
+        stage2(i).wait_send()
+        for d in (1, 2, 3):
+            stage3(i, d).wait_send()
+    for d, e in far_first:
+        last("z", d, e).wait_send()
+        last("y", d, e).wait_send()
 
 
 def body(images, projections, noise_power, class_logprior, groups, offsets):
@@ -467,16 +490,15 @@
             pltpu.VMEM((4, 2 * NX, ROWS, BLOCK), f32),
             pltpu.VMEM((2, 4, ROWS, BLOCK), bf16),
             pltpu.VMEM((2 * NX, 4, ROWS, BLOCK), bf16),
-            pltpu.VMEM((NZ, NY, OWN, WA), bf16),
-            pltpu.VMEM((NY, NZ, OWN, WB), bf16),
-            pltpu.VMEM((NZ, NY, OWN, WA), bf16),
-            pltpu.VMEM((NY, NZ, OWN, WB), bf16),
-            pltpu.VMEM((NY, OWN, WA), bf16),
-            pltpu.VMEM((NZ, OWN, WB), bf16),
-            pltpu.VMEM((NY, OWN, WA), bf16),
-            pltpu.VMEM((NZ, OWN, WB), bf16),
-            pltpu.VMEM((NX, 2, W), f32),
-            pltpu.VMEM((NX, 2, W), f32),
+            pltpu.VMEM((4 * BLOCK, ALL), bf16),
+            [pltpu.VMEM((2, 2, 4, 4, OWN, t[3]), bf16) for t in STREAMS],
+            [pltpu.VMEM((2, 4, 4, OWN, t[3]), bf16) for t in STREAMS],
+            [pltpu.VMEM((2, 4, 4, OWN, t[3]), bf16) for t in STREAMS],
+            [pltpu.VMEM((4, 4, OWN, t[3]), bf16) for t in STREAMS],
+            [pltpu.VMEM((4, 4, OWN, t[3]), bf16) for t in STREAMS],
+            [pltpu.VMEM((3, 4, OWN, t[3]), bf16) for t in STREAMS],
+            [pltpu.VMEM((4, NX, 2, t), bf16) for t in (WA, WB)],
+            [pltpu.VMEM((4, NX, 2, t), bf16) for t in (WA, WB)],
             dma((4,)),
             dma((2 * NX,)), dma((2 * NX,)),
             dma((6,)), dma((6,)),
@@ -484,8 +506,8 @@
             dma((2, 6)), dma((2, 6)),
             dma((4, 2 * NX)), dma((4, 2 * NX)),
             dma((2 * NX,)), dma((2 * NX,)),
-            dma((4, 8)), dma((4, 8)),
-            dma((NX,)), dma((NX,)),
+            dma((5, len(STREAMS))), dma((5, len(STREAMS))),
+            dma((2, 16)), dma((2, 16)),
         ],
         compiler_params=pltpu.CompilerParams(
             collective_id=0, has_side_effects=True, vmem_limit_bytes=58 * 1024 * 1024

time: 90.4 us -> 82.2 us (0.909)
  Pallas kernels: 89.6 us -> 81.3 us
    pallas_call x1, Pallas kernels: 88.1 us -> 79.8 us  [body(): pl.pallas_call(kernel, out_shape=(jax.ShapeDtypeStruct((NX, 2, W), f32),...]
where the time goes in v4:
time: 82.2 us; the launch traced here: 82 us
  Pallas kernels  81.3 us (99%)
    pallas_call x1, Pallas kernels, body(): pl.pallas_call(kernel, out_shape=(jax.ShapeDtypeStruct((NX, 2, W), f32),...  79.8 us

profile of v4, /device:TPU:8, one launch (start us, length us, event | category | flops | bytes accessed | tf_op | source)
XLA Modules:
  0.0 82.0 jit_solution(7328343465231171964)
XLA Ops:
  0.6 79.8 %estep.1 = (f32[4,2,1920]{2,1,0:T(2,128)}, f32[1,56]{1,0:T(1,128)}) custom-call(bf16[56,7200]{1,0:T(8,128)(2,1)} %img_hbm.1, bf16[30,240,128]{2,1,0:T(8,128)(2,1)} %bitcast.7, f32[32,7200]{1,0:T(8,128)} %noise_hbm.1, f32[1,4]{1,0:T(1,128)} %bitcast.8, s32[1,56]{1,0:T(1,128)} %bitcast.9, s32[1,56]{1,0:T(1,128)} %bitcast.10), custom_call_target="tpu_custom_call" | custom-call | tf_op jit(solution)/shard_map/estep/pallas_call | solution.py:472
  80.5 1.5 %finish.1 = (f32[2,7200]{1,0:T(2,128)}, f32[1,56]{1,0:T(1,128)}) custom-call(f32[4,2,1920]{2,1,0:T(2,128)} %get-tuple-element.6.fin_ref, f32[1,56]{1,0:T(1,128)} %get-tuple-element.7.ev_ref), custom_call_target="tpu_custom_call" | custom-call | tf_op jit(solution)/shard_map/finish/pallas_call | solution.py:520

commit v5 on v4

--- a/solution.py
+++ b/solution.py
@@ -44,7 +44,7 @@
     img_hbm, proj_hbm, noise_hbm, prior_ref, group_ref, offset_ref, out_ref, ev_ref,
     img_v, noise_v, img_ref, xin, white, inv3, pbuf, qbuf, sc_send, sc_recv, post_send, post_recv,
     wt, parts, in1, mid1, in2, mid2, in3, own, got,
-    load, img_s, img_r, cross_s, cross_r, pair_s, pair_r, side_s, side_r, sc_s, sc_r, post_s, post_r,
+    near_up, near_down, load, img_s, img_r, cross_s, cross_r, pair_s, pair_r, side_s, side_r, sc_s, sc_r, post_s, post_r,
     st_s, st_r, own_s, own_r,
 ):
     cls = lax.axis_index("cls")
@@ -98,10 +98,6 @@
     barrier = pltpu.get_barrier_semaphore()
     partners = [group(s // 2, s % 2) for s in range(1, 2 * NX)]
     partners += [along_y(1), along_y(NY - 1), along_z(1), along_z(NZ - 1)]
-    for d in (2, 4, 6):
-        for e in range(NX):
-            partners += [device((y + d) % NY, z, (x + e) % NX, c)]
-            partners += [device(y, (z + d) % NZ, (x + e) % NX, c)]
     for to in partners:
         pl.semaphore_signal(barrier, inc=1, device_id=to, device_id_type=pl.DeviceIdType.MESH)
 
@@ -183,8 +179,28 @@
         s = 2 * p + 1
         return copy(src, xin.at[s], img_s.at[s], img_r.at[s], group(0, 1))
 
+    def tell(r):
+        for n, at in ((0, along_y), (1, along_z)):
+            pl.semaphore_signal(
+                near_up.at[n, r - 1], inc=1, device_id=at(1), device_id_type=pl.DeviceIdType.MESH
+            )
+            if r <= 2:
+                pl.semaphore_signal(
+                    near_down.at[n, r - 1], inc=1, device_id=at(7),
+                    device_id_type=pl.DeviceIdType.MESH,
+                )
+
+    def told(r):
+        for n in (0, 1):
+            pl.semaphore_wait(near_up.at[n, r - 1], 1)
+            if r <= 2:
+                pl.semaphore_wait(near_down.at[n, r - 1], 1)
+        if r < 4:
+            tell(r + 1)
+
     for m in range(CHUNKS):
         to_across(m).start()
+    tell(1)
     for p in (1, 2, 3):
         image(p).start()
     to_sibling(0).start()
@@ -269,24 +285,26 @@
     columns(0)
     crossed(0)
     crossed(1)
+    told(1)
     crossed(2)
     paired(0)
     crossed(3)
-    paired(1)
+    told(2)
     image_arrived(1)
     image_arrived(2)
+    paired(1)
     whiten(2)
     whiten(4)
-    paired(2)
-    crossed(4)
     for s in (1, 3, 5):
         to_sibling(s // 2).wait_recv()
         whiten(s)
+    paired(2)
+    scores(0, 0, EARLY)
+    crossed(4)
     paired(3)
-    scores(0, 0, EARLY)
-    crossed(5)
     for m in range(CHUNKS):
         sided(0, m)
+    crossed(5)
     columns(1)
     scores(1, 0, EARLY)
     paired(4)
@@ -296,6 +314,7 @@
         sided(1, m)
     columns(2)
     paired(5)
+    told(3)
     to_sibling(3).wait_recv()
     whiten(7)
     scores(0, EARLY, 2 * NX)
@@ -304,6 +323,7 @@
     for m in (CHUNKS, CHUNKS + 1):
         sided(0, m)
         sided(1, m)
+    told(4)
     columns(3)
     scores(3, 0, 2 * NX)
 
@@ -499,6 +519,8 @@
             [pltpu.VMEM((3, 4, OWN, t[3]), bf16) for t in STREAMS],
             [pltpu.VMEM((4, NX, 2, t), bf16) for t in (WA, WB)],
             [pltpu.VMEM((4, NX, 2, t), bf16) for t in (WA, WB)],
+            pltpu.SemaphoreType.REGULAR((2, 4)),
+            pltpu.SemaphoreType.REGULAR((2, 2)),
             dma((4,)),
             dma((2 * NX,)), dma((2 * NX,)),
             dma((6,)), dma((6,)),

time: 82.2 us -> 80.9 us (0.984)
  Pallas kernels: 81.3 us -> 80 us
    pallas_call x1, Pallas kernels: 79.8 us -> 78.6 us  [body(): pl.pallas_call(kernel, out_shape=(jax.ShapeDtypeStruct((NX, 2, W), f32),...]
where the time goes in v5:
time: 80.9 us; the launch traced here: 80.7 us
  Pallas kernels  80 us (99%)
    pallas_call x1, Pallas kernels, body(): pl.pallas_call(kernel, out_shape=(jax.ShapeDtypeStruct((NX, 2, W), f32),...  78.6 us

profile of v5, /device:TPU:8, one launch (start us, length us, event | category | flops | bytes accessed | tf_op | source)
XLA Modules:
  0.0 80.7 jit_solution(6199005324833185404)
XLA Ops:
  0.6 78.6 %estep.1 = (f32[4,2,1920]{2,1,0:T(2,128)}, f32[1,56]{1,0:T(1,128)}) custom-call(bf16[56,7200]{1,0:T(8,128)(2,1)} %img_hbm.1, bf16[30,240,128]{2,1,0:T(8,128)(2,1)} %bitcast.7, f32[32,7200]{1,0:T(8,128)} %noise_hbm.1, f32[1,4]{1,0:T(1,128)} %bitcast.8, s32[1,56]{1,0:T(1,128)} %bitcast.9, s32[1,56]{1,0:T(1,128)} %bitcast.10), custom_call_target="tpu_custom_call" | custom-call | tf_op jit(solution)/shard_map/estep/pallas_call | solution.py:492
  79.2 1.5 %finish.1 = (f32[2,7200]{1,0:T(2,128)}, f32[1,56]{1,0:T(1,128)}) custom-call(f32[4,2,1920]{2,1,0:T(2,128)} %get-tuple-element.6.fin_ref, f32[1,56]{1,0:T(1,128)} %get-tuple-element.7.ev_ref), custom_call_target="tpu_custom_call" | custom-call | tf_op jit(solution)/shard_map/finish/pallas_call | solution.py:542

commit v6 on v5

--- a/solution.py
+++ b/solution.py
@@ -41,10 +41,12 @@
 
 
 def kernel(
-    img_hbm, proj_hbm, noise_hbm, prior_ref, group_ref, offset_ref, out_ref, ev_ref,
+    img_hbm, proj_hbm, noise_hbm, prior_ref, group_ref, offset_ref, out_hbm, ev_hbm,
+    out_ref, ev_ref,
     img_v, noise_v, img_ref, xin, white, inv3, pbuf, qbuf, sc_send, sc_recv, post_send, post_recv,
     wt, parts, in1, mid1, in2, mid2, in3, own, got,
-    near_up, near_down, load, img_s, img_r, cross_s, cross_r, pair_s, pair_r, side_s, side_r, sc_s, sc_r, post_s, post_r,
+    near_up, near_down, load, img_s, img_r, ring_s, cross_r, pair_r, side_r, sc_s, sc_r,
+    post_s, post_r,
     st_s, st_r, own_s, own_r,
 ):
     cls = lax.axis_index("cls")
@@ -132,14 +134,14 @@
         src, dst = (pbuf.at[0, mine], pbuf.at[1, mine])
         if m >= CHUNKS:
             src, dst = (pbuf.at[2, mine], pbuf.at[3, mine])
-        return copy(src, dst, cross_s.at[m], cross_r.at[m], across)
+        return copy(src, dst, ring_s.at[0], cross_r.at[m], across)
 
     def from_across(m):
         return pbuf.at[1 if m < CHUNKS else 3, half * CHUNKS + turned(m, lo)]
 
     def to_beside(m):
         dst = pbuf.at[2 if m < CHUNKS else 3, half * CHUNKS + turned(m, lo)]
-        return copy(from_across(m), dst, pair_s.at[m], pair_r.at[m], beside)
+        return copy(from_across(m), dst, ring_s.at[1], pair_r.at[m], beside)
 
     def from_beside(m):
         return pbuf.at[2 if m < CHUNKS else 3, half * CHUNKS + turned(m, 1 - lo)]
@@ -148,36 +150,35 @@
         ref = from_across(m) if way == 0 else from_beside(m)
         up = 1 - 2 * (turned(m, lo if way == 0 else 1 - lo) // 2)
         to = device(y, (z + NZ + up) % NZ, x, c)
-        return copy(ref, ref, side_s.at[way, m], side_r.at[way, m], to)
-
-    def sided(way, m):
-        chunk = (1 - half) * CHUNKS + turned(m, lo if way == 0 else 1 - lo)
-        ref = pbuf.at[(1 + way) if m < CHUNKS else 3, chunk]
-        copy(ref, ref, side_s.at[way, m], side_r.at[way, m], along_z(1)).wait_recv()
+        return copy(ref, ref, ring_s.at[2 + way], side_r.at[way if m < CHUNKS else 2], to)
+
+    def sided(slot):
+        ref = pbuf.at[slot, pl.ds((1 - half) * CHUNKS, CHUNKS)]
+        copy(ref, ref, ring_s.at[2], side_r.at[slot - 1], along_z(1)).wait_recv()
 
     def crossed(m):
         ref = from_across(m)
-        copy(ref, ref, cross_s.at[m], cross_r.at[m], across).wait_recv()
+        copy(ref, ref, ring_s.at[0], cross_r.at[m], across).wait_recv()
         to_beside(m).start()
         to_side(0, m).start()
 
     def paired(m):
         ref = from_beside(m)
-        copy(ref, ref, pair_s.at[m], pair_r.at[m], beside).wait_recv()
+        copy(ref, ref, ring_s.at[1], pair_r.at[m], beside).wait_recv()
         if m < 2:
             to_across(CHUNKS + m).start()
         to_side(1, m).start()
 
     def image(p):
         return copy(
-            img_ref.at[(x + STEPS[p]) % NX], xin.at[2 * p], img_s.at[2 * p], img_r.at[2 * p],
+            img_ref.at[(x + STEPS[p]) % NX], xin.at[2 * p], img_s.at[0], img_r.at[2 * p],
             group(STEPS[p], 0),
         )
 
     def to_sibling(p):
         src = img_ref.at[x] if p == 0 else xin.at[2 * p]
         s = 2 * p + 1
-        return copy(src, xin.at[s], img_s.at[s], img_r.at[s], group(0, 1))
+        return copy(src, xin.at[s], img_s.at[1], img_r.at[s], group(0, 1))
 
     def tell(r):
         for n, at in ((0, along_y), (1, along_z)):
@@ -260,7 +261,7 @@
 
     def score_copy(slot, s):
         return copy(
-            sc_send.at[slot, s], sc_recv.at[slot, s], sc_s.at[slot, s], sc_r.at[slot, s],
+            sc_send.at[slot, s], sc_recv.at[slot, s], sc_s.at[slot], sc_r.at[slot],
             group((NX - STEPS[s // 2]) % NX, s % 2),
         )
 
@@ -302,16 +303,14 @@
     scores(0, 0, EARLY)
     crossed(4)
     paired(3)
-    for m in range(CHUNKS):
-        sided(0, m)
+    sided(1)
     crossed(5)
     columns(1)
     scores(1, 0, EARLY)
     paired(4)
     image_arrived(3)
     whiten(6)
-    for m in range(CHUNKS):
-        sided(1, m)
+    sided(2)
     columns(2)
     paired(5)
     told(3)
@@ -320,17 +319,15 @@
     scores(0, EARLY, 2 * NX)
     scores(1, EARLY, 2 * NX)
     scores(2, 0, 2 * NX)
-    for m in (CHUNKS, CHUNKS + 1):
-        sided(0, m)
-        sided(1, m)
+    sided(3)
     told(4)
     columns(3)
     scores(3, 0, 2 * NX)
 
     total = {}
     for slot in range(4):
-        for s in range(1, 2 * NX):
-            score_copy(slot, s).wait_recv()
+        ref = sc_recv.at[slot, pl.ds(1, 2 * NX - 1)]
+        copy(ref, ref, sc_s.at[slot], sc_r.at[slot], group(1, 0)).wait_recv()
         for dc in (0, 1):
             terms = [sc_send[slot, 0]] if dc == 0 else [sc_recv[slot, 1]]
             terms += [sc_recv[slot, 2 * dx + dc] for dx in range(1, NX)]
@@ -345,20 +342,23 @@
         mass = term if mass is None else mass + term
     evidence = peak + jnp.log(jnp.sum(mass, axis=1, keepdims=True))
     ev_ref[...] = jnp.transpose(jnp.broadcast_to(evidence, (ROWS, TAG)))[0:1, :]
+    store_ev = pltpu.make_async_copy(ev_ref, ev_hbm, load.at[4])
+    store_ev.start()
     for (slot, dc), value in total.items():
         post_send[dc, slot] = jnp.exp(value - evidence).astype(bf16)
 
     def post_copy(s):
         return copy(
-            post_send.at[s % 2], post_recv.at[s], post_s.at[s], post_r.at[s],
+            post_send.at[s % 2], post_recv.at[s], post_s.at[0], post_r.at[0],
             group(STEPS[s // 2], s % 2),
         )
 
     for s in (6, 7, 2, 4, 3, 5, 1):
         post_copy(s).start()
     post_recv[0] = post_send[0]
-    for s in (1, 2, 4, 3, 5, 6, 7):
-        post_copy(s).wait_recv()
+    posts = post_recv.at[pl.ds(1, 2 * NX - 1)]
+    all_posts = copy(posts, posts, post_s.at[0], post_r.at[0], group(1, 0))
+    all_posts.wait_recv()
 
     for slot in range(4):
         wt[BLOCK * slot : BLOCK * (slot + 1)] = jnp.transpose(post_recv[:, slot].reshape(ALL, BLOCK))
@@ -389,9 +389,12 @@
     def stage3(i, d):
         axis = STREAMS[i][0]
         return copy(
-            mid2[i].at[(place[axis] // 2 + d) % 4], in3[i].at[d - 1], st_s.at[1 + d, i],
-            st_r.at[1 + d, i], along(axis, 2 * d),
-        )
+            mid2[i].at[(place[axis] // 2 + d) % 4], in3[i].at[d - 1], st_s.at[2, i],
+            st_r.at[2, i], along(axis, 2 * d),
+        )
+
+    def all3(i):
+        return copy(in3[i], in3[i], st_s.at[2, i], st_r.at[2, i], along("z", 2))
 
     def last(axis, d, e):
         n = "zy".index(axis)
@@ -399,13 +402,16 @@
         to = device(at, z, (x + e) % NX, c) if axis == "z" else device(y, at, (x + e) % NX, c)
         return copy(
             own[n].at[(place[other[axis]] // 2 + d) % 4, (x + e) % NX], got[n].at[d, x],
-            own_s.at[n, 4 * d + e], own_r.at[n, 4 * d + e], to,
-        )
-
-    def last_in(axis, d, e):
-        n = "zy".index(axis)
-        ref = got[n].at[d, (x + NX - e) % NX]
-        return copy(ref, ref, own_s.at[n, 4 * d + e], own_r.at[n, 4 * d + e], group(1, 0))
+            own_s.at[n, d], own_r.at[n, d], to,
+        )
+
+    def self_copy(n, axis):
+        return pltpu.make_async_copy(
+            own[n].at[place[other[axis]] // 2, x], got[n].at[0, x], own_r.at[n, 0]
+        )
+
+    def last_in(n, d):
+        return copy(got[n].at[d], got[n].at[d], own_s.at[n, d], own_r.at[n, d], group(1, 0))
 
     order = range(len(STREAMS))
     for i in order:
@@ -445,44 +451,45 @@
             _, _, col, width = STREAMS[i]
             col -= WA * n
             acc = mid2[i][place[axis] // 2].astype(f32)
+            all3(i).wait_recv()
             for d in (1, 3, 2):
-                stage3(i, d).wait_recv()
                 acc += in3[i][d - 1].astype(f32)
             for k in range(NX):
                 own[n][:, k, :, col : col + width] = acc[:, 2 * k : 2 * k + 2].astype(bf16)
         for d, e in far_first:
             last(axis, d, e).start()
-        got[n][0, x] = own[n][place[other[axis]] // 2, x]
+        self_copy(n, axis).start()
     for axis in "zy":
         n = "zy".index(axis)
-        for d, e in reversed(far_first):
-            last_in(axis, d, e).wait_recv()
+        for d in (0, 1, 3, 2):
+            last_in(n, d).wait_recv()
         acc = got[n][0].astype(f32)
         for d in range(1, 4):
             acc += got[n][d].astype(f32)
         out_ref[:, :, WA * n : WA * n + (WA, WB)[n]] = acc
-
-    for m in range(6):
-        to_across(m).wait_send()
-        to_beside(m).wait_send()
-        to_side(0, m).wait_send()
-        to_side(1, m).wait_send()
-    for p in range(NX):
-        if p:
-            image(p).wait_send()
-        to_sibling(p).wait_send()
-    for s in range(1, 2 * NX):
-        for slot in range(4):
-            score_copy(slot, s).wait_send()
-        post_copy(s).wait_send()
+    store_out = pltpu.make_async_copy(out_ref, out_hbm, load.at[5])
+    store_out.start()
+
+    def sent(ref, sem):
+        copy(ref, ref, sem, cross_r.at[0], across).wait_send()
+
+    for n in range(4):
+        sent(pbuf.at[n, pl.ds(0, 6)], ring_s.at[n])
+    sent(xin.at[pl.ds(0, NX - 1)], img_s.at[0])
+    sent(xin.at[pl.ds(0, NX)], img_s.at[1])
+    for slot in range(4):
+        sent(sc_send.at[slot, pl.ds(1, 2 * NX - 1)], sc_s.at[slot])
+    all_posts.wait_send()
     for i in order:
         stage1(i).wait_send()
         stage2(i).wait_send()
+        all3(i).wait_send()
+    for n in range(2):
+        sent(own[n].at[0, pl.ds(0, NX - 1)], own_s.at[n, 0])
         for d in (1, 2, 3):
-            stage3(i, d).wait_send()
-    for d, e in far_first:
-        last("z", d, e).wait_send()
-        last("y", d, e).wait_send()
+            sent(own[n].at[d], own_s.at[n, d])
+    store_ev.wait()
+    store_out.wait()
 
 
 def body(images, projections, noise_power, class_logprior, groups, offsets):
@@ -496,8 +503,10 @@
             jax.ShapeDtypeStruct((1, ROWS), f32),
         ),
         in_specs=[anywhere] * 3 + [pl.BlockSpec(memory_space=pltpu.SMEM), vmem, vmem],
-        out_specs=(vmem, vmem),
+        out_specs=(anywhere, anywhere),
         scratch_shapes=[
+            pltpu.VMEM((NX, 2, W), f32),
+            pltpu.VMEM((1, ROWS), f32),
             pltpu.VMEM((ROWS, F), bf16),
             pltpu.VMEM((GROUPS, F), f32),
             pltpu.VMEM((NX, ROWS, W + TAG), bf16),
@@ -521,15 +530,13 @@
             [pltpu.VMEM((4, NX, 2, t), bf16) for t in (WA, WB)],
             pltpu.SemaphoreType.REGULAR((2, 4)),
             pltpu.SemaphoreType.REGULAR((2, 2)),
-            dma((4,)),
-            dma((2 * NX,)), dma((2 * NX,)),
-            dma((6,)), dma((6,)),
-            dma((6,)), dma((6,)),
-            dma((2, 6)), dma((2, 6)),
-            dma((4, 2 * NX)), dma((4, 2 * NX)),
-            dma((2 * NX,)), dma((2 * NX,)),
-            dma((5, len(STREAMS))), dma((5, len(STREAMS))),
-            dma((2, 16)), dma((2, 16)),
+            dma((6,)),
+            dma((2,)), dma((2 * NX,)),
+            dma((4,)), dma((6,)), dma((6,)), dma((3,)),
+            dma((4,)), dma((4,)),
+            dma((1,)), dma((1,)),
+            dma((3, len(STREAMS))), dma((3, len(STREAMS))),
+            dma((2, 4)), dma((2, 4)),
         ],
         compiler_params=pltpu.CompilerParams(
             collective_id=0, has_side_effects=True, vmem_limit_bytes=58 * 1024 * 1024

time: 80.9 us -> 79 us (0.977)
  Pallas kernels: 80 us -> 78.2 us
    pallas_call x1, Pallas kernels: 78.6 us -> 76.7 us  [body(): pl.pallas_call(kernel, out_shape=(jax.ShapeDtypeStruct((NX, 2, W), f32),...]
where the time goes in v6:
time: 79 us; the launch traced here: 78.8 us
  Pallas kernels  78.2 us (99%)
    pallas_call x1, Pallas kernels, body(): pl.pallas_call(kernel, out_shape=(jax.ShapeDtypeStruct((NX, 2, W), f32),...  76.7 us

profile of v6, /device:TPU:8, one launch (start us, length us, event | category | flops | bytes accessed | tf_op | source)
XLA Modules:
  0.0 78.8 jit_solution(3653490931000665246)
XLA Ops:
  0.6 76.7 %estep.1 = (f32[4,2,1920]{2,1,0:T(2,128)}, f32[1,56]{1,0:T(1,128)}) custom-call(bf16[56,7200]{1,0:T(8,128)(2,1)} %img_hbm.1, bf16[30,240,128]{2,1,0:T(8,128)(2,1)} %bitcast.7, f32[32,7200]{1,0:T(8,128)} %noise_hbm.1, f32[1,4]{1,0:T(1,128)} %bitcast.8, s32[1,56]{1,0:T(1,128)} %bitcast.9, s32[1,56]{1,0:T(1,128)} %bitcast.10), custom_call_target="tpu_custom_call" | custom-call | tf_op jit(solution)/shard_map/estep/pallas_call | solution.py:499
  77.3 1.5 %finish.1 = (f32[2,7200]{1,0:T(2,128)}, f32[1,56]{1,0:T(1,128)}) custom-call(f32[4,2,1920]{2,1,0:T(2,128)} %get-tuple-element.6.fin_ref, f32[1,56]{1,0:T(1,128)} %get-tuple-element.7.ev_ref), custom_call_target="tpu_custom_call" | custom-call | tf_op jit(solution)/shard_map/finish/pallas_call | solution.py:549

commit v7 on v6

--- a/solution.py
+++ b/solution.py
@@ -33,11 +33,22 @@
 bf16 = jnp.bfloat16
 
 
-def finish(fin_ref, ev_ref, out_ref, evidence_ref):
+def finish(fin_hbm, ev_hbm, out_hbm, evidence_hbm, fin_ref, ev_ref, out_ref, sem):
+    load_fin = pltpu.make_async_copy(fin_hbm, fin_ref, sem.at[0])
+    load_ev = pltpu.make_async_copy(ev_hbm, ev_ref, sem.at[1])
+    store_ev = pltpu.make_async_copy(ev_ref, evidence_hbm, sem.at[2])
+    store_out = pltpu.make_async_copy(out_ref, out_hbm, sem.at[3])
+    load_fin.start()
+    load_ev.start()
+    load_ev.wait()
+    store_ev.start()
+    load_fin.wait()
     for k in range(NX):
         end = min(F, W * (k + 1))
         out_ref[:, W * k : end] = fin_ref[k, :, : end - W * k]
-    evidence_ref[...] = ev_ref[...]
+    store_out.start()
+    store_ev.wait()
+    store_out.wait()
 
 
 def kernel(
@@ -306,18 +317,18 @@
     sided(1)
     crossed(5)
     columns(1)
+    image_arrived(3)
     scores(1, 0, EARLY)
+    whiten(6)
     paired(4)
-    image_arrived(3)
-    whiten(6)
+    to_sibling(3).wait_recv()
+    whiten(7)
+    paired(5)
+    scores(0, EARLY, 2 * NX)
+    scores(1, EARLY, 2 * NX)
+    told(3)
     sided(2)
     columns(2)
-    paired(5)
-    told(3)
-    to_sibling(3).wait_recv()
-    whiten(7)
-    scores(0, EARLY, 2 * NX)
-    scores(1, EARLY, 2 * NX)
     scores(2, 0, 2 * NX)
     sided(3)
     told(4)
@@ -552,8 +563,14 @@
             jax.ShapeDtypeStruct((2, F), f32),
             jax.ShapeDtypeStruct((1, ROWS), f32),
         ),
-        in_specs=[vmem, vmem],
-        out_specs=(vmem, vmem),
+        in_specs=[anywhere, anywhere],
+        out_specs=(anywhere, anywhere),
+        scratch_shapes=[
+            pltpu.VMEM((NX, 2, W), f32),
+            pltpu.VMEM((1, ROWS), f32),
+            pltpu.VMEM((2, F), f32),
+            dma((4,)),
+        ],
         name="finish",
     )(out, evidence)
     return (out, evidence.reshape(ROWS))

time: 79 us -> 78 us (0.987)
  Pallas kernels: 78.2 us -> 77.2 us
    pallas_call x1, Pallas kernels: 76.7 us -> 75.7 us  [body(): pl.pallas_call(kernel, out_shape=(jax.ShapeDtypeStruct((NX, 2, W), f32),...]
where the time goes in v7:
time: 78 us; the launch traced here: 77.8 us
  Pallas kernels  77.2 us (99%)
    pallas_call x1, Pallas kernels, body(): pl.pallas_call(kernel, out_shape=(jax.ShapeDtypeStruct((NX, 2, W), f32),...  75.7 us

profile of v7, /device:TPU:8, one launch (start us, length us, event | category | flops | bytes accessed | tf_op | source)
XLA Modules:
  0.0 77.8 jit_solution(2444638114251497713)
XLA Ops:
  0.6 75.7 %estep.1 = (f32[4,2,1920]{2,1,0:T(2,128)}, f32[1,56]{1,0:T(1,128)}) custom-call(bf16[56,7200]{1,0:T(8,128)(2,1)} %img_hbm.1, bf16[30,240,128]{2,1,0:T(8,128)(2,1)} %bitcast.7, f32[32,7200]{1,0:T(8,128)} %noise_hbm.1, f32[1,4]{1,0:T(1,128)} %bitcast.8, s32[1,56]{1,0:T(1,128)} %bitcast.9, s32[1,56]{1,0:T(1,128)} %bitcast.10), custom_call_target="tpu_custom_call" | custom-call | tf_op jit(solution)/shard_map/estep/pallas_call | solution.py:510
  76.3 1.5 %finish.1 = (f32[2,7200]{1,0:T(2,128)}, f32[1,56]{1,0:T(1,128)}) custom-call(f32[4,2,1920]{2,1,0:T(2,128)} %get-tuple-element.6.fin_hbm, f32[1,56]{1,0:T(1,128)} %get-tuple-element.7.ev_hbm), custom_call_target="tpu_custom_call" | custom-call | tf_op jit(solution)/shard_map/finish/pallas_call | solution.py:560

commit v8 on v7

--- a/solution.py
+++ b/solution.py
@@ -52,8 +52,8 @@
 
 
 def kernel(
-    img_hbm, proj_hbm, noise_hbm, prior_ref, group_ref, offset_ref, out_hbm, ev_hbm,
-    out_ref, ev_ref,
+    img_hbm, proj_hbm, noise_hbm, prior_hbm, group_hbm, offset_hbm, out_hbm, ev_hbm,
+    prior_ref, group_ref, offset_ref, out_ref, ev_ref,
     img_v, noise_v, img_ref, xin, white, inv3, pbuf, qbuf, sc_send, sc_recv, post_send, post_recv,
     wt, parts, in1, mid1, in2, mid2, in3, own, got,
     near_up, near_down, load, img_s, img_r, ring_s, cross_r, pair_r, side_r, sc_s, sc_r,
@@ -89,7 +89,17 @@
             device_id=to, device_id_type=pl.DeviceIdType.MESH,
         )
 
-    load_img = pltpu.make_async_copy(img_hbm, img_v, load.at[0])
+    load_tags = [
+        pltpu.make_async_copy(group_hbm, group_ref, load.at[6]),
+        pltpu.make_async_copy(offset_hbm, offset_ref, load.at[7]),
+    ]
+    load_prior = pltpu.make_async_copy(prior_hbm, prior_ref, load.at[8])
+
+    def load_img(k):
+        lanes = pl.ds(W * k, min(F, W * (k + 1)) - W * k)
+        dst = img_ref.at[k, :, pl.ds(0, W)] if k < NX - 1 else img_v
+        return pltpu.make_async_copy(img_hbm.at[:, lanes], dst, load.at[9 + k])
+
     load_noise = pltpu.make_async_copy(noise_hbm, noise_v, load.at[1])
 
     load_proj = pltpu.make_async_copy(
@@ -99,14 +109,17 @@
         proj_hbm.at[pl.ds((x % (NX - 1)) * PARTS + WHOLE, PARTS - WHOLE)],
         pbuf.at[0, pl.ds(WHOLE, PARTS - WHOLE)], load.at[3],
     )
-    load_img.start()
+    for one in load_tags:
+        one.start()
     load_proj.start()
 
     @pl.when(x < NX - 1)
     def _():
         load_rest.start()
 
-    load_noise.start()
+    for k in range(NX):
+        load_img(k).start()
+    load_prior.start()
 
     barrier = pltpu.get_barrier_semaphore()
     partners = [group(s // 2, s % 2) for s in range(1, 2 * NX)]
@@ -114,16 +127,14 @@
     for to in partners:
         pl.semaphore_signal(barrier, inc=1, device_id=to, device_id_type=pl.DeviceIdType.MESH)
 
+    img_ref[NX - 1, :, LAST:W] = jnp.zeros((ROWS, W - LAST), bf16)
     tag = lax.broadcasted_iota(jnp.int32, (TAG, ROWS), 0)
+    for one in load_tags:
+        one.wait()
     is_group = (tag < 96) & (tag % 32 == group_ref[...])
     is_offset = (tag >= 96) & (tag < 108) & (tag % 4 == offset_ref[...])
     tags = jnp.transpose(jnp.where(is_group | is_offset, 1.0, 0.0).astype(f32)).astype(bf16)
-    load_img.wait()
     for k in range(NX):
-        end = min(F, W * (k + 1))
-        img_ref[k, :, : end - W * k] = img_v[:, W * k : end]
-        if end - W * k < W:
-            img_ref[k, :, end - W * k : W] = jnp.zeros((ROWS, W * (k + 1) - end), bf16)
         img_ref[k, :, W:] = tags
     load_proj.wait()
 
@@ -134,6 +145,12 @@
     @pl.when(x == NX - 1)
     def _():
         pbuf[0, WHOLE:] = jnp.zeros((PARTS - WHOLE, CHUNK, BLOCK), bf16)
+
+    for k in range(NX):
+        load_img(k).wait()
+    img_ref[NX - 1, :, :LAST] = img_v[...]
+    load_noise.start()
+    load_prior.wait()
 
     pl.semaphore_wait(barrier, len(partners))
 
@@ -506,19 +523,21 @@
 def body(images, projections, noise_power, class_logprior, groups, offsets):
     dma = pltpu.SemaphoreType.DMA
     anywhere = pl.BlockSpec(memory_space=pl.ANY)
-    vmem = pl.BlockSpec(memory_space=pltpu.VMEM)
     out, evidence = pl.pallas_call(
         kernel,
         out_shape=(
             jax.ShapeDtypeStruct((NX, 2, W), f32),
             jax.ShapeDtypeStruct((1, ROWS), f32),
         ),
-        in_specs=[anywhere] * 3 + [pl.BlockSpec(memory_space=pltpu.SMEM), vmem, vmem],
+        in_specs=[anywhere] * 6,
         out_specs=(anywhere, anywhere),
         scratch_shapes=[
+            pltpu.SMEM((1, CLASSES), f32),
+            pltpu.VMEM((1, ROWS), jnp.int32),
+            pltpu.VMEM((1, ROWS), jnp.int32),
             pltpu.VMEM((NX, 2, W), f32),
             pltpu.VMEM((1, ROWS), f32),
-            pltpu.VMEM((ROWS, F), bf16),
+            pltpu.VMEM((ROWS, LAST), bf16),
             pltpu.VMEM((GROUPS, F), f32),
             pltpu.VMEM((NX, ROWS, W + TAG), bf16),
             pltpu.VMEM((2 * NX, ROWS, W + TAG), bf16),
@@ -541,7 +560,7 @@
             [pltpu.VMEM((4, NX, 2, t), bf16) for t in (WA, WB)],
             pltpu.SemaphoreType.REGULAR((2, 4)),
             pltpu.SemaphoreType.REGULAR((2, 2)),
-            dma((6,)),
+            dma((9 + NX,)),
             dma((2,)), dma((2 * NX,)),
             dma((4,)), dma((6,)), dma((6,)), dma((3,)),
             dma((4,)), dma((4,)),

time: 78 us -> 77.4 us (level)
  no operation moved by 1% of the time
where the time goes in v8:
time: 77.4 us; the launch traced here: 77.2 us
  Pallas kernels  76.6 us (99%)
    pallas_call x1, Pallas kernels, body(): pl.pallas_call(kernel, out_shape=(jax.ShapeDtypeStruct((NX, 2, W), f32),...  75.1 us

profile of v8, /device:TPU:8, one launch (start us, length us, event | category | flops | bytes accessed | tf_op | source)
XLA Modules:
  0.0 77.2 jit_solution(5986932888460843243)
XLA Ops:
  0.6 75.1 %estep.1 = (f32[4,2,1920]{2,1,0:T(2,128)}, f32[1,56]{1,0:T(1,128)}) custom-call(bf16[56,7200]{1,0:T(8,128)(2,1)} %img_hbm.1, bf16[30,240,128]{2,1,0:T(8,128)(2,1)} %bitcast.7, f32[32,7200]{1,0:T(8,128)} %noise_hbm.1, f32[1,4]{1,0:T(1,128)} %bitcast.8, s32[1,56]{1,0:T(1,128)} %bitcast.9, s32[1,56]{1,0:T(1,128)} %bitcast.10), custom_call_target="tpu_custom_call" | custom-call | tf_op jit(solution)/shard_map/estep/pallas_call | solution.py:526
  75.7 1.5 %finish.1 = (f32[2,7200]{1,0:T(2,128)}, f32[1,56]{1,0:T(1,128)}) custom-call(f32[4,2,1920]{2,1,0:T(2,128)} %get-tuple-element.6.fin_hbm, f32[1,56]{1,0:T(1,128)} %get-tuple-element.7.ev_hbm), custom_call_target="tpu_custom_call" | custom-call | tf_op jit(solution)/shard_map/finish/pallas_call | solution.py:579

commit v9 on v8

--- a/solution.py
+++ b/solution.py
@@ -18,6 +18,7 @@
 WHOLE = F // CHUNK - (NX - 1) * PARTS
 STEPS = (0, 1, 3, 2)
 EARLY = 6
+PARTED = ((0, 32), (32, 24))
 LAST = F - (NX - 1) * W
 WA = 1024
 WB = W - WA
@@ -293,6 +294,13 @@
             group((NX - STEPS[s // 2]) % NX, s % 2),
         )
 
+    def score_part(n, s):
+        rows = pl.ds(*PARTED[n])
+        return copy(
+            sc_send.at[3, s, rows], sc_recv.at[3, s, rows], sc_s.at[3 + n], sc_r.at[3 + n],
+            group((NX - STEPS[s // 2]) % NX, s % 2),
+        )
+
     def scores(slot, first, last):
         rows = (last - first) * ROWS
         part = lax.dot_general(
@@ -302,6 +310,11 @@
             xin[first:last, :, W:].reshape(rows, TAG), qbuf[slot], NN, preferred_element_type=f32
         )
         sc_send[slot, first:last] = part.reshape(last - first, ROWS, BLOCK)
+        if slot == 3:
+            for n in range(2):
+                for s in (6, 7, 2, 4, 3, 5, 1):
+                    score_part(n, s).start()
+            return
         for s in (6, 7, 2, 4, 3, 5, 1):
             if first <= s < last:
                 score_copy(slot, s).start()
@@ -352,41 +365,58 @@
     columns(3)
     scores(3, 0, 2 * NX)
 
-    total = {}
-    for slot in range(4):
+    def all_scores(slot, n=0):
         ref = sc_recv.at[slot, pl.ds(1, 2 * NX - 1)]
-        copy(ref, ref, sc_s.at[slot], sc_r.at[slot], group(1, 0)).wait_recv()
-        for dc in (0, 1):
-            terms = [sc_send[slot, 0]] if dc == 0 else [sc_recv[slot, 1]]
-            terms += [sc_recv[slot, 2 * dx + dc] for dx in range(1, NX)]
-            total[slot, dc] = (terms[0] + terms[1]) + (terms[2] + terms[3])
-    peak = None
-    for value in total.values():
-        peak = value if peak is None else jnp.maximum(peak, value)
-    peak = jnp.max(peak, axis=1, keepdims=True)
-    mass = None
-    for value in total.values():
-        term = jnp.exp(value - peak)
-        mass = term if mass is None else mass + term
-    evidence = peak + jnp.log(jnp.sum(mass, axis=1, keepdims=True))
-    ev_ref[...] = jnp.transpose(jnp.broadcast_to(evidence, (ROWS, TAG)))[0:1, :]
+        if slot == 3:
+            ref = sc_recv.at[slot, pl.ds(1, 2 * NX - 1), pl.ds(*PARTED[n])]
+        return copy(ref, ref, sc_s.at[slot + n], sc_r.at[slot + n], group(1, 0))
+
+    def post_copy(n, s):
+        rows = pl.ds(*PARTED[n])
+        return copy(
+            post_send.at[s % 2, :, rows], post_recv.at[s, :, rows], post_s.at[n], post_r.at[n],
+            group(STEPS[s // 2], s % 2),
+        )
+
+    def all_posts(n):
+        ref = post_recv.at[pl.ds(1, 2 * NX - 1), :, pl.ds(*PARTED[n])]
+        return copy(ref, ref, post_s.at[n], post_r.at[n], group(1, 0))
+
+    for slot in range(3):
+        all_scores(slot).wait_recv()
+    evidences = []
+    for n in range(2):
+        first, rows = PARTED[n]
+        here = slice(first, first + rows)
+        all_scores(3, n).wait_recv()
+        total = {}
+        for slot in range(4):
+            for dc in (0, 1):
+                terms = [sc_send[slot, 0, here]] if dc == 0 else [sc_recv[slot, 1, here]]
+                terms += [sc_recv[slot, 2 * dx + dc, here] for dx in range(1, NX)]
+                total[slot, dc] = (terms[0] + terms[1]) + (terms[2] + terms[3])
+        peak = None
+        for value in total.values():
+            peak = value if peak is None else jnp.maximum(peak, value)
+        peak = jnp.max(peak, axis=1, keepdims=True)
+        mass = None
+        for value in total.values():
+            term = jnp.exp(value - peak)
+            mass = term if mass is None else mass + term
+        evidence = peak + jnp.log(jnp.sum(mass, axis=1, keepdims=True))
+        evidences.append(evidence)
+        for (slot, dc), value in total.items():
+            post_send[dc, slot, here] = jnp.exp(value - evidence).astype(bf16)
+        for s in (6, 7, 2, 4, 3, 5, 1):
+            post_copy(n, s).start()
+
+    evidence = jnp.broadcast_to(jnp.concatenate(evidences, axis=0), (ROWS, TAG))
+    ev_ref[...] = jnp.transpose(evidence)[0:1, :]
     store_ev = pltpu.make_async_copy(ev_ref, ev_hbm, load.at[4])
     store_ev.start()
-    for (slot, dc), value in total.items():
-        post_send[dc, slot] = jnp.exp(value - evidence).astype(bf16)
-
-    def post_copy(s):
-        return copy(
-            post_send.at[s % 2], post_recv.at[s], post_s.at[0], post_r.at[0],
-            group(STEPS[s // 2], s % 2),
-        )
-
-    for s in (6, 7, 2, 4, 3, 5, 1):
-        post_copy(s).start()
     post_recv[0] = post_send[0]
-    posts = post_recv.at[pl.ds(1, 2 * NX - 1)]
-    all_posts = copy(posts, posts, post_s.at[0], post_r.at[0], group(1, 0))
-    all_posts.wait_recv()
+    for n in range(2):
+        all_posts(n).wait_recv()
 
     for slot in range(4):
         wt[BLOCK * slot : BLOCK * (slot + 1)] = jnp.transpose(post_recv[:, slot].reshape(ALL, BLOCK))
@@ -505,9 +535,11 @@
         sent(pbuf.at[n, pl.ds(0, 6)], ring_s.at[n])
     sent(xin.at[pl.ds(0, NX - 1)], img_s.at[0])
     sent(xin.at[pl.ds(0, NX)], img_s.at[1])
-    for slot in range(4):
-        sent(sc_send.at[slot, pl.ds(1, 2 * NX - 1)], sc_s.at[slot])
-    all_posts.wait_send()
+    for slot in range(3):
+        all_scores(slot).wait_send()
+    for n in range(2):
+        all_scores(3, n).wait_send()
+        all_posts(n).wait_send()
     for i in order:
         stage1(i).wait_send()
         stage2(i).wait_send()
@@ -563,8 +595,8 @@
             dma((9 + NX,)),
             dma((2,)), dma((2 * NX,)),
             dma((4,)), dma((6,)), dma((6,)), dma((3,)),
-            dma((4,)), dma((4,)),
-            dma((1,)), dma((1,)),
+            dma((5,)), dma((5,)),
+            dma((2,)), dma((2,)),
             dma((3, len(STREAMS))), dma((3, len(STREAMS))),
             dma((2, 4)), dma((2, 4)),
         ],

time: 77.4 us -> 76.5 us (0.988)
  Pallas kernels: 76.6 us -> 75.7 us
    pallas_call x1, Pallas kernels: 75.1 us -> 74.2 us  [body(): pl.pallas_call(kernel, out_shape=(jax.ShapeDtypeStruct((NX, 2, W), f32),...]
where the time goes in v9:
time: 76.5 us; the launch traced here: 76.3 us
  Pallas kernels  75.7 us (99%)
    pallas_call x1, Pallas kernels, body(): pl.pallas_call(kernel, out_shape=(jax.ShapeDtypeStruct((NX, 2, W), f32),...  74.2 us

profile of v9, /device:TPU:8, one launch (start us, length us, event | category | flops | bytes accessed | tf_op | source)
XLA Modules:
  0.0 76.3 jit_solution(2923344485616298561)
XLA Ops:
  0.6 74.2 %estep.1 = (f32[4,2,1920]{2,1,0:T(2,128)}, f32[1,56]{1,0:T(1,128)}) custom-call(bf16[56,7200]{1,0:T(8,128)(2,1)} %img_hbm.1, bf16[30,240,128]{2,1,0:T(8,128)(2,1)} %bitcast.7, f32[32,7200]{1,0:T(8,128)} %noise_hbm.1, f32[1,4]{1,0:T(1,128)} %bitcast.8, s32[1,56]{1,0:T(1,128)} %bitcast.9, s32[1,56]{1,0:T(1,128)} %bitcast.10), custom_call_target="tpu_custom_call" | custom-call | tf_op jit(solution)/shard_map/estep/pallas_call | solution.py:558
  74.8 1.5 %finish.1 = (f32[2,7200]{1,0:T(2,128)}, f32[1,56]{1,0:T(1,128)}) custom-call(f32[4,2,1920]{2,1,0:T(2,128)} %get-tuple-element.6.fin_hbm, f32[1,56]{1,0:T(1,128)} %get-tuple-element.7.ev_hbm), custom_call_target="tpu_custom_call" | custom-call | tf_op jit(solution)/shard_map/finish/pallas_call | solution.py:611

commit v10 on v9

--- a/solution.py
+++ b/solution.py
@@ -91,15 +91,15 @@
         )
 
     load_tags = [
-        pltpu.make_async_copy(group_hbm, group_ref, load.at[6]),
-        pltpu.make_async_copy(offset_hbm, offset_ref, load.at[7]),
+        pltpu.make_async_copy(group_hbm, group_ref, load.at[7]),
+        pltpu.make_async_copy(offset_hbm, offset_ref, load.at[8]),
     ]
-    load_prior = pltpu.make_async_copy(prior_hbm, prior_ref, load.at[8])
+    load_prior = pltpu.make_async_copy(prior_hbm, prior_ref, load.at[9])
 
     def load_img(k):
         lanes = pl.ds(W * k, min(F, W * (k + 1)) - W * k)
         dst = img_ref.at[k, :, pl.ds(0, W)] if k < NX - 1 else img_v
-        return pltpu.make_async_copy(img_hbm.at[:, lanes], dst, load.at[9 + k])
+        return pltpu.make_async_copy(img_hbm.at[:, lanes], dst, load.at[10 + k])
 
     load_noise = pltpu.make_async_copy(noise_hbm, noise_v, load.at[1])
 
@@ -269,9 +269,10 @@
         square = p * p
         s_hi = square.astype(bf16)
         s_lo = (square - s_hi.astype(f32)).astype(bf16)
-        q = lax.dot_general(inv3[...], s_hi, NN, preferred_element_type=f32)
-        q += lax.dot_general(inv3[...], s_lo, NN, preferred_element_type=f32)
+        both = jnp.concatenate([s_hi, s_lo], axis=1)
+        q = lax.dot_general(inv3[: 3 * GROUPS], both, NN, preferred_element_type=f32)
         q = q[0:32] + q[32:64] + q[64:96]
+        q = q[:, :BLOCK] + q[:, BLOCK:]
         prior = jnp.zeros((TAG, BLOCK), f32)
         for o in range(CLASSES):
             log_prior = prior_ref[0, (h + turn[slot] + CLASSES - o) % CLASSES]
@@ -501,22 +502,27 @@
         for d in (2, 1, 3):
             stage3(i, d).start()
     far_first = [(d, e) for d in (2, 1, 3, 0) for e in (2, 1, 3, 0) if d or e]
-    for axis in "zy":
+    for i in order:
+        axis, _, col, width = STREAMS[i]
         n = "zy".index(axis)
-        for i in order:
-            if STREAMS[i][0] != axis:
-                continue
-            _, _, col, width = STREAMS[i]
-            col -= WA * n
-            acc = mid2[i][place[axis] // 2].astype(f32)
-            all3(i).wait_recv()
-            for d in (1, 3, 2):
-                acc += in3[i][d - 1].astype(f32)
-            for k in range(NX):
-                own[n][:, k, :, col : col + width] = acc[:, 2 * k : 2 * k + 2].astype(bf16)
-        for d, e in far_first:
-            last(axis, d, e).start()
-        self_copy(n, axis).start()
+        col -= WA * n
+        acc = mid2[i][place[axis] // 2].astype(f32)
+        all3(i).wait_recv()
+        for d in (1, 3, 2):
+            acc += in3[i][d - 1].astype(f32)
+        for k in range(NX):
+            own[n][:, k, :, col : col + width] = acc[:, 2 * k : 2 * k + 2].astype(bf16)
+        if all(t[0] != axis for t in STREAMS[i + 1 :]):
+            for d, e in far_first:
+                last(axis, d, e).start()
+            self_copy(n, axis).start()
+
+    def store_out(n):
+        lanes = pl.ds(WA * n, (WA, WB)[n])
+        return pltpu.make_async_copy(
+            out_ref.at[:, :, lanes], out_hbm.at[:, :, lanes], load.at[5 + n]
+        )
+
     for axis in "zy":
         n = "zy".index(axis)
         for d in (0, 1, 3, 2):
@@ -525,8 +531,7 @@
         for d in range(1, 4):
             acc += got[n][d].astype(f32)
         out_ref[:, :, WA * n : WA * n + (WA, WB)[n]] = acc
-    store_out = pltpu.make_async_copy(out_ref, out_hbm, load.at[5])
-    store_out.start()
+        store_out(n).start()
 
     def sent(ref, sem):
         copy(ref, ref, sem, cross_r.at[0], across).wait_send()
@@ -549,7 +554,8 @@
         for d in (1, 2, 3):
             sent(own[n].at[d], own_s.at[n, d])
     store_ev.wait()
-    store_out.wait()
+    store_out(0).wait()
+    store_out(1).wait()
 
 
 def body(images, projections, noise_power, class_logprior, groups, offsets):
@@ -592,7 +598,7 @@
             [pltpu.VMEM((4, NX, 2, t), bf16) for t in (WA, WB)],
             pltpu.SemaphoreType.REGULAR((2, 4)),
             pltpu.SemaphoreType.REGULAR((2, 2)),
-            dma((9 + NX,)),
+            dma((10 + NX,)),
             dma((2,)), dma((2 * NX,)),
             dma((4,)), dma((6,)), dma((6,)), dma((3,)),
             dma((5,)), dma((5,)),

time: 76.5 us -> 77.4 us (1.012)
  Pallas kernels: 75.7 us -> 76.5 us
    pallas_call x1, Pallas kernels: 74.2 us -> 75 us  [body(): pl.pallas_call(kernel, out_shape=(jax.ShapeDtypeStruct((NX, 2, W), f32),...]
where the time goes in v10:
time: 77.4 us; the launch traced here: 77.2 us
  Pallas kernels  76.5 us (99%)
    pallas_call x1, Pallas kernels, body(): pl.pallas_call(kernel, out_shape=(jax.ShapeDtypeStruct((NX, 2, W), f32),...  75 us

profile of v10, /device:TPU:8, one launch (start us, length us, event | category | flops | bytes accessed | tf_op | source)
XLA Modules:
  0.0 77.2 jit_solution(8764908672765845070)
XLA Ops:
  0.6 75.0 %estep.1 = (f32[4,2,1920]{2,1,0:T(2,128)}, f32[1,56]{1,0:T(1,128)}) custom-call(bf16[56,7200]{1,0:T(8,128)(2,1)} %img_hbm.1, bf16[30,240,128]{2,1,0:T(8,128)(2,1)} %bitcast.7, f32[32,7200]{1,0:T(8,128)} %noise_hbm.1, f32[1,4]{1,0:T(1,128)} %bitcast.8, s32[1,56]{1,0:T(1,128)} %bitcast.9, s32[1,56]{1,0:T(1,128)} %bitcast.10), custom_call_target="tpu_custom_call" | custom-call | tf_op jit(solution)/shard_map/estep/pallas_call | solution.py:564
  75.7 1.5 %finish.1 = (f32[2,7200]{1,0:T(2,128)}, f32[1,56]{1,0:T(1,128)}) custom-call(f32[4,2,1920]{2,1,0:T(2,128)} %get-tuple-element.6.fin_hbm, f32[1,56]{1,0:T(1,128)} %get-tuple-element.7.ev_hbm), custom_call_target="tpu_custom_call" | custom-call | tf_op jit(solution)/shard_map/finish/pallas_call | solution.py:617
